TPU v7x, 8 devices: a whole 2x2x1 slice. The times are simulated.
8 devices in a mesh: b: 4 (over z, y, x), a: 2 (over core).
Axes of the slice: x: 2, y: 2, z: 1, core: 2. Of those that a mesh axis runs over, the one named last changes fastest.
Arguments:
- u: float32 [256, 256, 256], P(None, 'a', 'b')
- g: float32 [130, 256, 256], P('a', 'b')
Outputs:
- output: float32 [256, 256, 256], P(None, 'a', 'b')
All inputs are finite; a program needn't handle non-finite values.
Results may differ from a plain program's by a relative error of at most 0.001.
Values are sent between devices in bfloat16 or wider.
A program may use at most 1 GiB of HBM per device.

v0:
```python
import math
import functools
import jax
import jax.numpy as jnp
from jax import lax
from jax.sharding import PartitionSpec as P

HI = lax.Precision.HIGHEST


def _trig(n, rows, cols):
    r = jnp.arange(rows, dtype=jnp.int32)[:, None]
    c = jnp.arange(cols, dtype=jnp.int32)[None, :]
    ang = ((r * c) % n).astype(jnp.float32) * (2.0 * math.pi / n)
    return jnp.cos(ang), jnp.sin(ang)


def _xtables(n, kx):
    cx, sx = _trig(n, kx, n)
    k = jnp.arange(kx)
    keep = (k <= n // 2).astype(jnp.float32)
    wgt = jnp.where((k == 0) | (k == n // 2), 1.0, 2.0) * keep / n
    return cx * keep[:, None], -sx * keep[:, None], (cx * wgt[:, None]).T, (sx * wgt[:, None]).T


def _mm(p, q):
    return jnp.dot(p, q, precision=HI, preferred_element_type=jnp.float32)


def _line(x, c, s, form, sign):
    e = functools.partial(jnp.einsum, form, precision=HI, preferred_element_type=jnp.float32)
    return jnp.stack([e(x[0], c) + sign * e(x[1], s), e(x[1], c) - sign * e(x[0], s)])


def solution(mesh):
    na = mesh.shape["a"]

    def local(u, g):
        n, ya, zb = u.shape
        kx = g.shape[0] * na
        c1, s1, ar, ai = _xtables(n, kx)
        c, s = _trig(n, n, n)
        ci, si = c / n, s / n
        u2 = u.reshape(n, ya * zb)
        x = jnp.stack([_mm(c1, u2), _mm(s1, u2)]).reshape(2, kx, ya, zb)
        x = lax.all_to_all(x, "a", 1, 2, tiled=True)
        x = _line(x, c, s, "xyz,yk->xkz", 1.0)
        x = lax.all_to_all(x, "b", 2, 3, tiled=True)
        x = _line(x, c, s, "xyz,zk->xyk", 1.0) * g[None]
        x = _line(x, ci, si, "xyz,zk->xyk", -1.0)
        x = lax.all_to_all(x, "b", 3, 2, tiled=True)
        x = _line(x, ci, si, "xyz,yk->xkz", -1.0)
        x = lax.all_to_all(x, "a", 2, 1, tiled=True)
        w = _mm(ar, x[0].reshape(kx, ya * zb)) - _mm(ai, x[1].reshape(kx, ya * zb))
        return w.reshape(n, ya, zb)

    return jax.shard_map(local, mesh=mesh, in_specs=(P(None, "a", "b"), P("a", "b", None)), out_specs=P(None, "a", "b"), check_vma=False)
```

profile of v0, /device:TPU:0, one launch (start us, length us, event | category | flops | bytes accessed | tf_op | source)
XLA Modules:
  0.0 924.5 jit_solution(580498025323179031)
XLA Ops:
  0.0 9.2 copy.64
  9.2 13.2 %convolution_bitcast_fusion = f32[1,130,128,64]{2,1,3,0:T(8,128)S(1)} fusion(f32[128,64,256]{2,0,1:T(8,128)} %copy.64, f32[130]{0:T(256)S(1)} %fusion.98), kind=kOutput, calls=%fused_computation.20 | convolution fusion | flops 3272089600 | bytes 12648968 | tf_op jit(solution)/shard_map/dot_general | solution.py:27
  22.4 9.5 %convolution_bitcast_fusion.1 = f32[1,130,128,64]{2,1,3,0:T(8,128)S(1)} fusion(f32[128,64,256]{2,0,1:T(8,128)S(1)} %copy-done, f32[130]{0:T(256)S(1)} %fusion.98), kind=kOutput, calls=%fused_computation.21 | convolution fusion | flops 3272056320 | bytes 12648968 | tf_op jit(solution)/shard_map/dot_general | solution.py:27
  31.9 0.6 pad_maximum_fusion.2
  32.4 1.6 copy.66
  34.1 12.4 %all_to_all.60 = f32[2,130,128,64]{2,3,0,1:T(8,128)} all-to-all(f32[2,130,128,64]{2,3,0,1:T(8,128)S(1)} %copy.66), channel_id=1, replica_groups=mesh['b'=4,'a'=2] {'a'}, dimensions={1} | all-to-all | bytes 17039360 | tf_op jit(solution)/shard_map/all_to_all | solution.py:46
  46.5 4.3 copy.67
  50.8 3.3 fusion.194
  54.1 5.3 copy.97
  59.4 7.0 reshape.155
  66.4 0.0 slice-start.7
  66.4 9.5 %fusion.21 = f32[256,65,64]{0,1,2:T(8,128)} fusion(f32[65,256,64]{1,0,2:T(8,128)} %reshape.155), kind=kOutput, calls=%fused_computation.42 | convolution fusion | flops 3272474624 | bytes 8519680 | tf_op jit(solution)/shard_map/xyz,yk->xkz/dot_general | solution.py:32
  76.0 5.4 copy.98
  81.3 6.6 reshape.156
  88.0 8.4 fusion.19
  96.4 8.1 add_bitcast_fusion.1
  104.5 5.4 subtract_bitcast_fusion.1
  109.9 4.4 pad_maximum_fusion
  114.3 14.4 %copy.74 = f32[2,65,256,64]{1,3,0,2:T(8,128)} copy(f32[2,65,256,64]{2,1,3,0:T(8,128)} %pad_maximum_fusion) | data formatting | bytes 17039360 | tf_op jit(solution)/shard_map/stack | solution.py:32
  128.7 195.5 %all_to_all.61 = f32[2,65,256,64]{1,3,0,2:T(8,128)} all-to-all(f32[2,65,256,64]{1,3,0,2:T(8,128)} %copy.74), channel_id=1, replica_groups=mesh['b'=4,'a'=2] {'b'}, dimensions={2} | all-to-all | bytes 17039360 | tf_op jit(solution)/shard_map/all_to_all | solution.py:48
  324.3 21.9 %copy.94 = f32[2,65,4,64,64]{3,2,4,1,0:T(4,128)} copy(f32[2,65,4,64,64]{1,4,0,3,2:T(8,128)} %bitcast.137) | data formatting | bytes 17039360 | tf_op jit(solution)/shard_map/all_to_all | solution.py:48
  346.2 14.4 %fusion.192 = (f32[1,65,64,4,64]{2,3,4,1,0:T(4,128)}, f32[1,65,64,4,64]{2,3,4,1,0:T(4,128)}) fusion(f32[2,65,64,4,64]{2,3,4,1,0:T(4,128)} %bitcast.135), kind=kLoop, calls=%fused_computation.202 | loop fusion | bytes 17039360 | tf_op jit(solution)/shard_map/slice | solution.py:32
  360.6 12.1 %copy.76 = f32[1,65,64,4,64]{4,3,2,1,0:T(4,128)} copy(f32[1,65,64,4,64]{2,3,4,1,0:T(4,128)} %get-tuple-element.7) | data formatting | bytes 8519680 | tf_op jit(solution)/shard_map/slice | solution.py:32
  372.7 8.7 squeeze.34
  381.3 8.6 fusion.17
  390.0 12.1 %copy.77 = f32[1,65,64,4,64]{4,3,2,1,0:T(4,128)} copy(f32[1,65,64,4,64]{2,3,4,1,0:T(4,128)} %get-tuple-element.8) | data formatting | bytes 8519680 | tf_op jit(solution)/shard_map/slice | solution.py:32
  402.1 8.6 squeeze.35
  410.7 7.8 fusion.15
  418.6 0.0 slice-start.8
  418.6 9.0 add_bitcast_fusion.3
  427.7 0.0 slice-start.9
  427.7 4.9 subtract_bitcast_fusion.3
  432.6 2.4 maximum_multiply_fusion
  435.1 4.6 fusion.1
  439.7 4.5 fusion
  444.2 5.1 add_bitcast_fusion.2
  449.3 4.8 subtract_bitcast_fusion.2
  454.1 4.3 pad_maximum_fusion.3
  458.4 14.2 %copy.78 = f32[2,65,64,256]{1,2,0,3:T(8,128)} copy(f32[2,65,64,256]{3,2,1,0:T(8,128)} %pad_maximum_fusion.3) | data formatting | bytes 17039360 | tf_op jit(solution)/shard_map/stack | solution.py:32
  472.6 7.4 all-to-all-start.2
  480.0 181.7 %all-to-all-done.2 = f32[2,65,64,256]{1,2,0,3:T(8,128)} async-done(((f32[2,65,64,256]{1,2,0,3:T(8,128)}), f32[2,65,64,256]{1,2,0,3:T(8,128)}, u32[]{:S(2)}, u32[]{:S(2)}) %all-to-all-start.2) | async-done | bytes 8519712 | tf_op jit(solution)/shard_map/all_to_all | solution.py:51
  661.7 21.9 %copy.95 = f32[2,65,64,4,64]{4,3,2,1,0:T(4,128)} copy(f32[2,65,64,4,64]{1,2,0,4,3:T(8,128)} %bitcast.32) | data formatting | bytes 17039360 | tf_op jit(solution)/shard_map/all_to_all | solution.py:51
  683.6 14.4 %fusion.191 = (f32[1,65,4,64,64]{4,2,3,1,0:T(4,128)}, f32[1,65,4,64,64]{4,2,3,1,0:T(4,128)}) fusion(f32[2,65,4,64,64]{4,2,3,1,0:T(4,128)} %bitcast.136), kind=kLoop, calls=%fused_computation.201 | loop fusion | bytes 17039360 | tf_op jit(solution)/shard_map/slice | solution.py:32
  698.0 11.7 %copy.101 = f32[1,65,4,64,64]{3,2,1,4,0:T(4,128)} copy(f32[1,65,4,64,64]{4,2,3,1,0:T(4,128)} %get-tuple-element.5) | data formatting | bytes 8519680 | tf_op jit(solution)/shard_map/squeeze | solution.py:32
  709.7 9.3 %reshape.157 = f32[65,256,64]{1,0,2:T(8,128)} reshape(f32[1,65,4,64,64]{3,2,1,4,0:T(4,128)} %copy.101) | data formatting | bytes 8519680 | tf_op jit(solution)/shard_map/squeeze | solution.py:32
  719.0 9.5 %fusion.25 = f32[256,65,64]{0,1,2:T(8,128)} fusion(f32[65,256,64]{1,0,2:T(8,128)} %reshape.157), kind=kOutput, calls=%fused_computation.46 | convolution fusion | flops 3272540160 | bytes 8519680 | tf_op jit(solution)/shard_map/xyz,yk->xkz/dot_general | solution.py:32
  728.4 11.7 %copy.102 = f32[1,65,4,64,64]{3,2,1,4,0:T(4,128)} copy(f32[1,65,4,64,64]{4,2,3,1,0:T(4,128)} %get-tuple-element.6) | data formatting | bytes 8519680 | tf_op jit(solution)/shard_map/squeeze | solution.py:32
  740.1 9.3 %reshape.158 = f32[65,256,64]{1,0,2:T(8,128)} reshape(f32[1,65,4,64,64]{3,2,1,4,0:T(4,128)} %copy.102) | data formatting | bytes 8519680 | tf_op jit(solution)/shard_map/squeeze | solution.py:32
  749.4 8.3 fusion.23
  757.8 8.2 add_bitcast_fusion
  766.0 5.6 subtract_bitcast_fusion
  771.6 4.4 pad_maximum_fusion.1
  776.0 14.4 %copy.86 = f32[2,65,256,64]{1,3,0,2:T(8,128)} copy(f32[2,65,256,64]{2,1,3,0:T(8,128)} %pad_maximum_fusion.1) | data formatting | bytes 17039360 | tf_op jit(solution)/shard_map/stack | solution.py:32
  790.3 31.5 %all_to_all.62 = f32[2,65,256,64]{1,3,0,2:T(8,128)} all-to-all(f32[2,65,256,64]{1,3,0,2:T(8,128)} %copy.86), channel_id=1, replica_groups=mesh['b'=4,'a'=2] {'a'}, dimensions={2} | all-to-all | bytes 17039360 | tf_op jit(solution)/shard_map/all_to_all | solution.py:53
  821.8 16.3 %copy.96 = f32[2,65,2,128,64]{3,2,4,1,0:T(2,128)} copy(f32[2,65,2,128,64]{1,4,0,3,2:T(8,128)} %bitcast.138) | data formatting | bytes 17039360 | tf_op jit(solution)/shard_map/all_to_all | solution.py:53
  838.1 13.3 %fusion.193 = (f32[1,2,65,128,64]{3,1,4,2,0:T(2,128)}, f32[1,2,65,128,64]{3,1,4,2,0:T(2,128)}) fusion(f32[2,2,65,128,64]{3,1,4,2,0:T(2,128)} %bitcast.142), kind=kLoop, calls=%fused_computation.203 | loop fusion | bytes 17039360 | tf_op jit(solution)/shard_map/slice | solution.py:54
  851.4 8.8 copy.88
  860.2 8.1 reshape_squeeze.6
  868.3 8.8 copy.89
  877.1 8.2 reshape_squeeze.7
  885.3 10.3 %fusion.57 = f32[256,8192]{1,0:T(8,128)S(1)} fusion(f32[130,8192]{1,0:T(8,128)} %reshape_squeeze.6, f32[130]{0:T(256)S(1)} %fusion.102), kind=kOutput, calls=%fused_computation.84 | convolution fusion | flops 3272056320 | bytes 12648968 | tf_op jit(solution)/shard_map/dot_general | solution.py:27
  895.5 10.8 %convolution_subtract_fusion = f32[256,8192]{1,0:T(8,128)} fusion(f32[256,8192]{1,0:T(8,128)S(1)} %fusion.57, f32[130,8192]{1,0:T(8,128)S(1)} %copy-done.4, f32[130]{0:T(256)S(1)} %fusion.102), kind=kOutput, calls=%fused_computation | convolution fusion | flops 3274153472 | bytes 21037576 | tf_op jit(solution)/shard_map/dot_general | solution.py:27
  906.3 9.1 copy.90
  915.4 8.8 copy.91
  (34 shorter events, 0.1 us)
Async XLA Ops:
  9.2 13.2 %copy-start = (f32[128,64,256]{2,0,1:T(8,128)S(1)}, f32[128,64,256]{2,0,1:T(8,128)}, u32[]{:S(2)}) copy-start(f32[128,64,256]{2,0,1:T(8,128)} %copy.64) | copy-start | bytes 25165828
  59.4 16.5 %slice-start.6 = ((s8[4259840]{0:T(1024)(128)(4,1)}), s8[65536]{0:T(1024)(128)(4,1)S(1)}, s32[]{:S(2)}) async-start(s8[4259840]{0:T(1024)(128)(4,1)} %bitcast.144), calls=%async_computation.10 | async-start | bytes 131072
  66.4 9.5 %slice-start.7 = ((s8[4259840]{0:T(1024)(128)(4,1)}), s8[4194304]{0:T(1024)(128)(4,1)S(1)}, s32[]{:S(2)}) async-start(s8[4259840]{0:T(1024)(128)(4,1)} %bitcast.144), calls=%async_computation.11 | async-start | bytes 8388608
  81.3 23.1 %slice-start.2 = ((s8[4718592]{0:T(1024)(128)(4,1)}), s8[524288]{0:T(1024)(128)(4,1)S(1)}, s32[]{:S(2)}) async-start(s8[4718592]{0:T(1024)(128)(4,1)} %bitcast.133), calls=%async_computation.6 | async-start | bytes 1048576
  88.0 8.4 copy-start.2
  88.0 16.5 %slice-start.3 = ((s8[4718592]{0:T(1024)(128)(4,1)}), s8[4194304]{0:T(1024)(128)(4,1)S(1)}, s32[]{:S(2)}) async-start(s8[4718592]{0:T(1024)(128)(4,1)} %bitcast.133), calls=%async_computation.7 | async-start | bytes 8388608
  410.7 7.9 copy-start.3
  410.7 16.9 %slice-start.4 = ((s8[4259840]{0:T(1024)(128)(4,1)}), s8[4194304]{0:T(1024)(128)(4,1)S(1)}, s32[]{:S(2)}) async-start(s8[4259840]{0:T(1024)(128)(4,1)} %bitcast.139), calls=%async_computation.8 | async-start | bytes 8388608
  418.6 9.1 slice-start.5
  418.6 14.0 %slice-start.8 = ((s8[4259840]{0:T(1024)(128)(4,1)}), s8[4194304]{0:T(1024)(128)(4,1)S(1)}, s32[]{:S(2)}) async-start(s8[4259840]{0:T(1024)(128)(4,1)} %bitcast.147), calls=%async_computation.12 | async-start | bytes 8388608
  427.7 5.0 slice-start.9
  472.6 189.1 %all-to-all-start.2 = ((f32[2,65,64,256]{1,2,0,3:T(8,128)}), f32[2,65,64,256]{1,2,0,3:T(8,128)}, u32[]{:S(2)}, u32[]{:S(2)}) async-start(f32[2,65,64,256]{1,2,0,3:T(8,128)} %copy.78), calls=%async_computation.2 | async-start | bytes 33554432 | tf_op jit(solution)/shard_map/all_to_all | solution.py:51
  740.1 25.8 %slice-start = ((s8[4718592]{0:T(1024)(128)(4,1)}), s8[524288]{0:T(1024)(128)(4,1)S(1)}, s32[]{:S(2)}) async-start(s8[4718592]{0:T(1024)(128)(4,1)} %bitcast.131), calls=%async_computation.4 | async-start | bytes 1048576
  749.4 8.3 copy-start.1
  749.4 16.5 %slice-start.1 = ((s8[4718592]{0:T(1024)(128)(4,1)}), s8[4194304]{0:T(1024)(128)(4,1)S(1)}, s32[]{:S(2)}) async-start(s8[4718592]{0:T(1024)(128)(4,1)} %bitcast.131), calls=%async_computation.5 | async-start | bytes 8388608
  885.2 10.3 %copy-start.4 = (f32[130,8192]{1,0:T(8,128)S(1)}, f32[130,8192]{1,0:T(8,128)}, u32[]{:S(2)}) copy-start(f32[130,8192]{1,0:T(8,128)} %reshape_squeeze.7) | copy-start | bytes 12779524
where the time goes:
time: 934 us; the launch traced here: 924 us
  local copies, waits for them, and re-layouts  323 us (35%)
  blocking collectives  239 us (26%)
  waiting for transfers between devices  182 us (19%)
  matrix products  156 us (17%)
  other arithmetic  16.1 us (2%)
    all_to_all x1, blocking collectives, local(): x = lax.all_to_all(x, 'b', 2, 3, tiled=True)  196 us
    all_to_all x1, waiting for transfers between devices, local(): x = lax.all_to_all(x, 'b', 3, 2, tiled=True)  182 us
    slice x4, local copies, waits for them, and re-layouts, _line(): x[0]  44.2 us
    dot_general x4, matrix products, _mm(): return jnp.dot(p, q, precision=HI, preferred_element_type=jnp.float32)  43.7 us
    another operation x3, local copies, waits for them, and re-layouts, _line(): jnp.stack([e(x[0], c) + sign * e(x[1], s), e(x[1], c) - sign * e(x[0], s)])  43 us
    squeeze x5, local copies, waits for them, and re-layouts, _line(): x[0]  41.9 us
    squeeze x5, local copies, waits for them, and re-layouts, _line(): x[1]  41.6 us
    dot_general x4, matrix products, _line(): e(x[0], c) + sign * e(x[1], s)  32.2 us
  transfers between devices with their start and end apart: 1, of which 1 were waited for; matrix products, arithmetic and copies ran while one was open for 0% of the time, Pallas kernels for 0%

commit v1 on v0

v1 whole, which is shorter than its diff:
```python
import functools
import math
import jax
import jax.numpy as jnp
import numpy as np
from jax import lax
from jax.experimental import pallas as pl
from jax.experimental.pallas import tpu as pltpu
from jax.sharding import PartitionSpec as P

HI = lax.Precision.HIGHEST
F32 = jnp.float32
KC = 5


def _trig(n, rows, cols):
    r = np.arange(rows)[:, None]
    c = np.arange(cols)[None, :]
    ang = ((r * c) % n).astype(np.float32) * np.float32(2.0 * math.pi / n)
    return np.cos(ang.astype(np.float64)), np.sin(ang.astype(np.float64))


def _xtables(n, kx, pad):
    cx, sx = _trig(n, kx, n)
    k = np.arange(kx)
    keep = (k <= n // 2).astype(np.float64)
    wgt = np.where((k == 0) | (k == n // 2), 1.0, 2.0) * keep / n
    fwd = np.zeros((pad, n))
    fwd[: 2 * kx] = np.stack([cx * keep[:, None], -sx * keep[:, None]], 1).reshape(2 * kx, n)
    inv = np.zeros((pad, n))
    inv[: 2 * kx] = np.stack([cx * wgt[:, None], -sx * wgt[:, None]], 1).reshape(2 * kx, n)
    return fwd.astype(np.float32), inv.T.astype(np.float32).copy()


def _ytables(n, nb):
    c, s = _trig(n, n, n)
    full = np.block([[c, -s], [s, c]])
    w = full.reshape(2 * n, 2, nb, n // nb).transpose(0, 2, 1, 3).reshape(2 * n, 2 * n)
    inv = (full.T / n).reshape(2, nb, n // nb, 2 * n).transpose(1, 0, 2, 3)
    inv = inv.reshape(2 * n, 2, 2, n // 2).transpose(0, 2, 1, 3).reshape(2 * n, 2 * n)
    return w.astype(np.float32), inv.astype(np.float32)


def _dot(p, q):
    return jnp.dot(p, q, precision=HI, preferred_element_type=F32)


def _xfwd(t_ref, u_ref, o_ref):
    x, zb, y = u_ref.shape
    k = o_ref.shape[0]
    src = u_ref.reshape(x * zb, y)
    dst = o_ref.reshape(k * zb, y)
    for z in range(0, zb, 2):
        rhs = jnp.concatenate([src[pl.ds(z + i, x, stride=zb), :] for i in range(2)], axis=1)
        out = _dot(t_ref[...], rhs)
        for i in range(2):
            dst[pl.ds(z + i, k, stride=zb), :] = out[:, i * y:(i + 1) * y]


def _spectral(nb, p_ref, g_ref, wy_ref, cs_ref, wi_ref, q_ref,
              xb, sf, r, v, qs, gv, csv, wiv,
              load_sem, xa_send, xa_recv, xl_sem, f_send, f_recv, b_send, b_recv, q_send, q_recv, ql_sem):
    b, a = lax.axis_index("b"), lax.axis_index("a")
    other = 1 - a
    nkx = g_ref.shape[0]
    nchunk = nkx // KC
    zb, n = r.shape[1] // nb, r.shape[1]
    bx, by = lax.rem(b, 2), lax.div(b, 2)
    peers = [lax.rem(by + d // 2, 2) * 2 + lax.rem(bx + d % 2, 2) for d in (1, 2, 3)]
    MESH = pl.DeviceIdType.MESH

    def ck(i):
        return pl.ds(i * KC, KC)

    def ck2(i):
        return pl.ds(i * 2 * KC, 2 * KC)

    def prow(owner, i):
        return p_ref.at[pl.ds(owner * 2 * nkx + i * 2 * KC, 2 * KC)]

    loads = [pltpu.make_async_copy(s, d, load_sem.at[i]) for i, (s, d) in enumerate(
        [(g_ref, gv), (cs_ref, csv), (wi_ref, wiv)])]

    def xlocal(i):
        return pltpu.make_async_copy(prow(a, i), xb.at[a, ck2(i)], xl_sem.at[i])

    def xremote(i):
        return pltpu.make_async_remote_copy(
            prow(other, i), xb.at[a, ck2(i)], xa_send.at[i], xa_recv.at[i],
            device_id=(b, other), device_id_type=MESH)

    def fwd(i, d):
        return pltpu.make_async_remote_copy(
            sf.at[ck(i), peers[d]], r.at[ck(i), pl.ds(b * zb, zb)], f_send.at[d, i], f_recv.at[d, i],
            device_id=(peers[d], a), device_id_type=MESH)

    def bwd(i, d):
        return pltpu.make_async_remote_copy(
            r.at[ck(i), pl.ds(peers[d] * zb, zb)], v.at[ck(i), b], b_send.at[d, i], b_recv.at[d, i],
            device_id=(peers[d], a), device_id_type=MESH)

    def qlocal(i):
        return pltpu.make_async_copy(qs.at[a, ck(i)], q_ref.at[a, ck(i)], ql_sem.at[i])

    def qremote(i):
        return pltpu.make_async_remote_copy(
            qs.at[other, ck(i)], q_ref.at[a, ck(i)], q_send.at[i], q_recv.at[i],
            device_id=(b, other), device_id_type=MESH)

    barrier = pltpu.get_barrier_semaphore()
    for dev in [(b, other)] + [(pb, a) for pb in peers]:
        pl.semaphore_signal(barrier, inc=1, device_id=dev, device_id_type=MESH)

    @pl.loop(0, nchunk)
    def _(i):
        xlocal(i).start()

    pl.semaphore_wait(barrier, 4)

    @pl.loop(0, nchunk)
    def _(i):
        xremote(i).start()

    for c in loads:
        c.start()

    @pl.loop(0, nchunk)
    def _(i):
        xlocal(i).wait()
        xremote(i).wait_recv()
        x = jnp.concatenate(
            [jnp.concatenate([xb[h, (i * KC + j) * 2 + c] for j in range(KC)]) for c in range(2) for h in range(2)], axis=1)
        out = _dot(x, wy_ref[...])
        for k in range(nb):
            sf[ck(i), k] = out[:, k * 128:(k + 1) * 128].reshape(KC, zb, 128)
        r[ck(i), pl.ds(b * zb, zb)] = sf[ck(i), b]
        for d in range(3):
            fwd(i, d).start()

    for c in loads:
        c.wait()
    lane = lax.broadcasted_iota(jnp.int32, (n, 128), 1)
    sign = jnp.where(lane < 64, 1.0, -1.0).astype(F32)

    @pl.loop(0, nchunk)
    def _(i):
        for d in range(3):
            fwd(i, d).wait_recv()

        def cat(parts):
            return jnp.concatenate(parts, axis=1)

        e = _dot(csv[...], cat([r[i * KC + j] for j in range(KC)]))
        parts = []
        for j in range(KC):
            cols = slice(j * 128, (j + 1) * 128)
            g1 = gv[i * KC + j] * (1.0 / n)
            gt = jnp.transpose(jnp.concatenate([g1, g1], axis=0))
            parts.append((e[:n, cols] + sign * pltpu.roll(e[n:, cols], 64, 1)) * gt)
        e = _dot(csv[...], cat(parts))
        for j in range(KC):
            cols = slice(j * 128, (j + 1) * 128)
            r[i * KC + j] = e[:n, cols] - sign * pltpu.roll(e[n:, cols], 64, 1)
        v[ck(i), b] = r[ck(i), pl.ds(b * zb, zb)]
        for d in range(3):
            bwd(i, d).start()

    @pl.loop(0, nchunk)
    def _(i):
        for d in range(3):
            bwd(i, d).wait_recv()
        x = jnp.concatenate([v[ck(i), k].reshape(KC * zb, 128) for k in range(nb)], axis=1)
        out = _dot(x, wiv[...])
        for h in range(2):
            for c in range(2):
                m = h * 2 + c
                qs[h, ck(i), c] = out[:, m * 128:(m + 1) * 128].reshape(KC, zb, 128)
        qremote(i).start()
        qlocal(i).start()

    @pl.loop(0, nchunk)
    def _(i):
        xremote(i).wait_send()
        for d in range(3):
            fwd(i, d).wait_send()
            bwd(i, d).wait_send()
        qlocal(i).wait()
        qremote(i).wait()


def _xinv(t_ref, q_ref, o_ref):
    k, zb, y = q_ref.shape
    x = o_ref.shape[0]
    src = q_ref.reshape(k * zb, y)
    dst = o_ref.reshape(x * zb, y)
    for z in range(0, zb, 2):
        rhs = jnp.concatenate([src[pl.ds(z + i, k, stride=zb), :] for i in range(2)], axis=1)
        out = _dot(t_ref[...], rhs)
        for i in range(2):
            dst[pl.ds(z + i, x, stride=zb), :] = out[:, i * y:(i + 1) * y]


def solution(mesh):
    na, nb = mesh.shape["a"], mesh.shape["b"]

    def local(u, g):
        n, ya, zb = u.shape
        nkx = g.shape[0]
        kx = nkx * na
        rows = 2 * kx
        pad = -(-rows // 8) * 8
        tf, ti = _xtables(n, kx, pad)
        wy, wi = _ytables(n, nb)
        c, s = _trig(n, n, n)
        cs = np.concatenate([c, s]).astype(np.float32)
        zt = 8
        ut = jnp.transpose(u, (0, 2, 1))
        vm = pltpu.CompilerParams(vmem_limit_bytes=60 << 20)
        p = pl.pallas_call(
            _xfwd, grid=(zb // zt,), name="xfwd",
            in_specs=[pl.BlockSpec((pad, n), lambda i: (0, 0)), pl.BlockSpec((n, zt, ya), lambda i: (0, i, 0))],
            out_specs=pl.BlockSpec((pad, zt, ya), lambda i: (0, i, 0)),
            out_shape=jax.ShapeDtypeStruct((pad, zb, ya), F32), compiler_params=vm,
        )(tf, ut)
        nchunk = nkx // KC
        anyspec = pl.BlockSpec(memory_space=pl.ANY)
        dma = pltpu.SemaphoreType.DMA
        q = pl.pallas_call(
            functools.partial(_spectral, nb), name="spectral",
            in_specs=[anyspec, anyspec, pl.BlockSpec(memory_space=pltpu.VMEM), anyspec, anyspec],
            out_specs=anyspec,
            out_shape=jax.ShapeDtypeStruct((na, nkx, 2, zb, ya), F32),
            scratch_shapes=[
                pltpu.VMEM((na, nkx * 2, zb, ya), F32),
                pltpu.VMEM((nkx, nb, zb, 128), F32),
                pltpu.VMEM((nkx, n, 128), F32),
                pltpu.VMEM((nkx, nb, zb, 128), F32),
                pltpu.VMEM((na, nkx, 2, zb, ya), F32),
                pltpu.VMEM(g.shape, F32), pltpu.VMEM(cs.shape, F32), pltpu.VMEM(wi.shape, F32),
                dma((3,)), dma((nchunk,)), dma((nchunk,)), dma((nchunk,)),
                dma((3, nchunk)), dma((3, nchunk)), dma((3, nchunk)), dma((3, nchunk)),
                dma((nchunk,)), dma((nchunk,)), dma((nchunk,)),
            ],
            compiler_params=pltpu.CompilerParams(
                collective_id=0, has_side_effects=True, vmem_limit_bytes=67043328),
        )(p, g, wy, cs, wi)
        w = pl.pallas_call(
            _xinv, grid=(zb // zt,), name="xinv",
            in_specs=[pl.BlockSpec((n, rows), lambda i: (0, 0)), pl.BlockSpec((rows, zt, ya), lambda i: (0, i, 0))],
            out_specs=pl.BlockSpec((n, zt, ya), lambda i: (0, i, 0)),
            out_shape=jax.ShapeDtypeStruct((n, zb, ya), F32), compiler_params=vm,
        )(ti[:, :rows], q.reshape(rows, zb, ya))
        return jnp.transpose(w, (0, 2, 1))

    return jax.shard_map(local, mesh=mesh, in_specs=(P(None, "a", "b"), P("a", "b", None)), out_specs=P(None, "a", "b"), check_vma=False)
```

time: 934 us -> 230 us (0.25)
  local copies, waits for them, and re-layouts: 323 us -> 0 us
  blocking collectives: 239 us -> 0 us
  Pallas kernels: 0 us -> 229 us
  waiting for transfers between devices: 182 us -> 0 us
  matrix products: 156 us -> 0 us
  other arithmetic: 16.1 us -> 0 us
    all_to_all x3 -> x0, blocking collectives: 239 us -> none  [the longest x1 196 us: local(): x = lax.all_to_all(x, 'b', 2, 3, tiled=True)]
    pallas_call x0 -> x3, Pallas kernels: none -> 229 us  [the longest x1 197 us: local(): pl.pallas_call(functools.partial(_spectral, nb), name='spectral', in_spec...]
    all_to_all x1 -> x0, waiting for transfers between devices: 182 us -> none  [local(): x = lax.all_to_all(x, 'b', 3, 2, tiled=True)]
    dot_general x20 -> x0, matrix products: 156 us -> none  [the longest x4 43.7 us: _mm(): return jnp.dot(p, q, precision=HI, preferred_element_type=jnp.float32)]
    slice x8 -> x0, local copies, waits for them, and re-layouts: 87.1 us -> none  [the longest x4 44.2 us: _line(): x[0]]
    squeeze x10 -> x0, local copies, waits for them, and re-layouts: 83.5 us -> none  [the longest x5 41.9 us: _line(): x[0]]
    all_to_all x4 -> x0, local copies, waits for them, and re-layouts: 64.4 us -> none  [the longest x1 21.9 us: local(): x = lax.all_to_all(x, 'b', 2, 3, tiled=True)]
    another operation x6 -> x0, local copies, waits for them, and re-layouts: 60.9 us -> none  [the longest x3 43 us: _line(): jnp.stack([e(x[0], c) + sign * e(x[1], s), e(x[1], c) - sign * e(x[0], s)])]
  transfers between devices with their start and end apart: 1 -> 0, of which waited for: 1 -> 0; matrix products, arithmetic and copies ran while one was open for 0% -> 0% of each run, Pallas kernels for 0% -> 0%
where the time goes in v1:
time: 230 us; the launch traced here: 229 us
  Pallas kernels  229 us (100%)
    pallas_call x1, Pallas kernels, local(): pl.pallas_call(functools.partial(_spectral, nb), name='spectral', in_spec...  197 us
    pallas_call x1, Pallas kernels, local(): pl.pallas_call(_xinv, grid=(zb // zt,), name='xinv', in_specs=[pl.BlockSp...  18.3 us
    pallas_call x1, Pallas kernels, local(): pl.pallas_call(_xfwd, grid=(zb // zt,), name='xfwd', in_specs=[pl.BlockSp...  13.6 us

profile of v1, /device:TPU:0, one launch (start us, length us, event | category | flops | bytes accessed | tf_op | source)
XLA Modules:
  0.0 229.4 jit_solution(950152758752282335)
XLA Ops:
  0.0 13.6 %xfwd.1.p_ref = f32[264,64,128]{2,1,0:T(8,128)} custom-call(f32[264,256]{1,0:T(8,128)} %constant.10.clone.t_ref, f32[256,64,128]{2,1,0:T(8,128)} %bitcast.4), custom_call_target="tpu_custom_call" | custom-call | tf_op jit(solution)/shard_map/xfwd/pallas_call | solution.py:219
  13.6 197.4 %spectral.1 = f32[2,65,2,64,128]{4,3,2,1,0:T(8,128)} custom-call(f32[264,64,128]{2,1,0:T(8,128)} %xfwd.1.p_ref, f32[65,64,256]{2,1,0:T(8,128)} %g_ref.1, f32[512,512]{1,0:T(8,128)} %constant.11.clone.wy_ref, f32[512,256]{1,0:T(8,128)} %constant.12.clone.cs_ref, f32[512,512]{1,0:T(8,128)} %constant.13.clone.wi_ref), custom_call_target="tpu_custom_call" | custom-call | tf_op jit(solution)/shard_map/spectral/pallas_call | solution.py:228
  211.1 18.3 %xinv.1 = f32[256,64,128]{2,1,0:T(8,128)} custom-call(f32[256,260]{1,0:T(8,128)} %constant.14.clone.t_ref, f32[260,64,128]{2,1,0:T(8,128)} %bitcast.3), custom_call_target="tpu_custom_call" | custom-call | tf_op jit(solution)/shard_map/xinv/pallas_call | solution.py:247

commit v2 on v0

v2 whole, which is shorter than its diff:
```python
import functools
import math
import jax
import jax.numpy as jnp
import numpy as np
from jax import lax
from jax.experimental import pallas as pl
from jax.experimental.pallas import tpu as pltpu
from jax.sharding import PartitionSpec as P

HI = lax.Precision.HIGHEST
F32, BF16 = jnp.float32, jnp.bfloat16
MESH = pl.DeviceIdType.MESH
KC = 5
KA = 13
NLAST = 2
ZT = 8
ROWS = 136
HALF = ROWS // 2
TROWS = 144


def _trig(n, rows, cols):
    r = np.arange(rows)[:, None]
    c = np.arange(cols)[None, :]
    ang = ((r * c) % n).astype(np.float32) * np.float32(2.0 * math.pi / n)
    return np.cos(ang.astype(np.float64)), np.sin(ang.astype(np.float64))


def _xforward(n, kx, na):
    cx, sx = _trig(n, kx, n)
    keep = (np.arange(kx) <= n // 2).astype(np.float64)[:, None]
    t = np.zeros((na, 2, HALF, n))
    t[:, 0, : kx // na] = (cx * keep).reshape(na, kx // na, n)
    t[:, 1, : kx // na] = (-sx * keep).reshape(na, kx // na, n)
    t = np.pad(t.reshape(na, ROWS, n), ((0, 0), (0, TROWS - ROWS), (0, 0)))
    return np.concatenate([t, t[:1]]).reshape((na + 1) * TROWS, n).astype(np.float32)


def _xinverse(n, kx, na):
    cx, sx = _trig(n, kx, n)
    k = np.arange(kx)
    wgt = (np.where((k == 0) | (k == n // 2), 1.0, 2.0) * (k <= n // 2) / n)[:, None]
    t = np.stack([cx * wgt, -sx * wgt], 1).reshape(na, kx // na // KC, KC, 2, n)
    return t.transpose(1, 0, 2, 3, 4).reshape(2 * kx, n).T.astype(np.float32).copy()


def _ytables(n, nb):
    c, s = _trig(n, n, n)
    full = np.block([[c, -s], [s, c]])
    w = full.reshape(2 * n, 2, nb, n // nb).transpose(0, 2, 1, 3).reshape(2 * n, 2 * n)
    inv = (full.T / n).reshape(2, nb, n // nb, 2 * n).transpose(1, 0, 2, 3)
    inv = inv.reshape(2 * n, 2, 2, n // 2).transpose(0, 2, 1, 3).reshape(2 * n, 2 * n)
    return w.astype(np.float32), inv.astype(np.float32)


def _split(x):
    hi = x.astype(BF16)
    x = x - hi.astype(F32)
    mid = x.astype(BF16)
    return hi, mid, (x - mid.astype(F32)).astype(BF16)


def _nsplit(x):
    hi = x.astype(jnp.bfloat16)
    x = x - hi.astype(np.float32)
    mid = x.astype(jnp.bfloat16)
    return hi, mid, (x - mid.astype(np.float32)).astype(jnp.bfloat16)


def _mm(p, q):
    d = functools.partial(jnp.dot, preferred_element_type=F32)
    return d(p[0], q[2]) + d(p[1], q[1]) + d(p[2], q[0]) + d(p[0], q[1]) + d(p[1], q[0]) + d(p[0], q[0])


def _dot(p, q):
    return jnp.dot(p, q, precision=HI, preferred_element_type=F32)


def _cat(parts):
    return jnp.concatenate(parts, axis=1)


def _spectral(nb, u_ref, g_ref, t_ref, wy_ref, cs_ref, wi_ref, ai_ref, acc_ref, ql_ref,
              uv, xb, ps, sf, r, v, qx, ws, gv, tv, wv, csv, aiv, tsp, wysp, wisp,
              load_sem, u_sem, g_sem, xa_send, xa_recv, fa_send, fa_recv, f_send, f_recv,
              b_send, b_recv, q_send, q_recv, ql_sem, w_sem):
    b, a = lax.axis_index("b"), lax.axis_index("a")
    other = 1 - a
    nkx = g_ref.shape[0]
    nchunk, npiece = nkx // KC, nkx // KA
    nbulk = nchunk - NLAST
    n = r.shape[1]
    zb = n // nb
    nz = zb // ZT
    y = 128
    bx, by = lax.rem(b, 2), lax.div(b, 2)
    peers = [lax.rem(by + d // 2, 2) * 2 + lax.rem(bx + d % 2, 2) for d in (1, 2, 3)]
    us = uv.shape[0]

    def ck(i):
        return pl.ds(i * KC, KC)

    def ka(i):
        return pl.ds(i * KA, KA)

    loads = [pltpu.make_async_copy(s, d, load_sem.at[i]) for i, (s, d) in enumerate(
        [(t_ref, tv), (wy_ref, wv), (wi_ref, wv), (cs_ref, csv), (ai_ref, aiv)])]
    gs = gv.shape[0]

    def gload(i):
        return pltpu.make_async_copy(g_ref.at[ck(i)], gv.at[lax.rem(i, gs)], g_sem.at[lax.rem(i, gs)])

    def uload(z):
        return pltpu.make_async_copy(
            u_ref.at[:, pl.ds(z * ZT, ZT)], uv.at[lax.rem(z, us)], u_sem.at[lax.rem(z, us)])

    def xremote(z):
        return pltpu.make_async_remote_copy(
            ps.at[z], xb.at[z, a], xa_send.at[z], xa_recv.at[z], device_id=(b, other), device_id_type=MESH)

    def fwda(i, d):
        return pltpu.make_async_remote_copy(
            sf.at[ka(i), peers[d], pl.ds(0, ZT)], r.at[ka(i), pl.ds(b * zb, ZT)],
            fa_send.at[d, i], fa_recv.at[d, i], device_id=(peers[d], a), device_id_type=MESH)

    def fwd(i, d):
        return pltpu.make_async_remote_copy(
            sf.at[ck(i), peers[d], pl.ds(ZT, zb - ZT)], r.at[ck(i), pl.ds(b * zb + ZT, zb - ZT)],
            f_send.at[d, i], f_recv.at[d, i], device_id=(peers[d], a), device_id_type=MESH)

    def bwd(i, d):
        return pltpu.make_async_remote_copy(
            r.at[ck(i), pl.ds(peers[d] * zb, zb)], v.at[ck(i), b], b_send.at[d, i], b_recv.at[d, i],
            device_id=(peers[d], a), device_id_type=MESH)

    def qsrc(i):
        return ps.at[:, pl.ds(i * 2 * KC, 2 * KC)]

    def qremote(i):
        return pltpu.make_async_remote_copy(
            qsrc(i), qx.at[:, i, a], q_send.at[i], q_recv.at[i], device_id=(b, other), device_id_type=MESH)

    def qlast(i):
        return pltpu.make_async_remote_copy(
            qsrc(i), ql_ref.at[:, i - nbulk, a], q_send.at[i], q_recv.at[i],
            device_id=(b, other), device_id_type=MESH)

    def qlocal(i):
        return pltpu.make_async_copy(qx.at[:, i, a], ql_ref.at[:, i - nbulk, a], ql_sem.at[i - nbulk])

    def wstore(z):
        return pltpu.make_async_copy(
            ws.at[lax.rem(z, 2)], acc_ref.at[pl.ds(z * ZT, ZT)], w_sem.at[lax.rem(z, 2)])

    barrier = pltpu.get_barrier_semaphore()
    for dev in [(b, other)] + [(pb, a) for pb in peers]:
        pl.semaphore_signal(barrier, inc=1, device_id=dev, device_id_type=MESH)
    loads[0].start()
    for z in range(us):
        uload(z).start()
    for c in (loads[1], loads[3], loads[4]):
        c.start()
    for i in range(gs):
        gload(i).start()

    src = uv.reshape(us * n * ZT, y)
    own = xb.reshape(nz * 2 * ROWS * ZT, y)
    sent = ps.reshape(nz * ROWS * ZT, y)

    def split_table(dst, step):
        @pl.loop(0, wv.shape[0] // step)
        def _(i):
            rows = pl.ds(i * step, step)
            for m, part in enumerate(_split(wv[rows, :])):
                dst[m, rows, :] = part

    def xhalf(zi, z, rhs, first, dst, base):
        rows = pl.ds(pl.multiple_of(first * TROWS, 16), TROWS)
        out = _mm([tsp[m, rows, :] for m in range(3)], rhs)
        for i in range(2):
            dst[pl.ds(base * ROWS * ZT + z + i, ROWS, stride=ZT), :] = out[:ROWS, i * y:(i + 1) * y]

    def xblock(zi, halves):
        slot = lax.rem(zi, us)
        for z in range(0, ZT, 2):
            rhs = _split(_cat([src[pl.ds(slot * n * ZT + z + i, n, stride=ZT), :] for i in range(2)]))
            if 1 in halves:
                xhalf(zi, z, rhs, a + 1, sent, zi)
            if 0 in halves:
                xhalf(zi, z, rhs, a, own, zi * 2 + a)

    loads[0].wait()
    for m, part in enumerate(_split(tv[...])):
        tsp[m] = part
    uload(0).wait()
    xblock(0, (1,))
    pl.semaphore_wait(barrier, 4)
    xremote(0).start()
    xblock(0, (0,))
    loads[1].wait()
    split_table(wysp, 128)
    loads[2].start()
    xremote(0).wait_recv()

    @pl.loop(0, npiece)
    def _(i):
        x = _split(_cat([xb[0, h, pl.ds(c * HALF + i * KA, KA)].reshape(KA * ZT, y)
                         for c in range(2) for h in range(2)]))
        out = _mm(x, [wysp[m] for m in range(3)])
        for k in range(nb):
            sf[ka(i), k, pl.ds(0, ZT)] = out[:, k * y:(k + 1) * y].reshape(KA, ZT, y)
        r[ka(i), pl.ds(b * zb, ZT)] = sf[ka(i), b, pl.ds(0, ZT)]
        for d in range(3):
            fwda(i, d).start()

    @pl.loop(1, nz)
    def _(z):
        @pl.when(z + us - 1 < nz)
        def _():
            uload(z + us - 1).start()
        uload(z).wait()
        xblock(z, (1, 0))
        xremote(z).start()

    @pl.loop(1, nz)
    def _(z):
        xremote(z).wait_recv()

    zr = zb - ZT

    @pl.loop(0, nchunk)
    def _(i):
        x = _cat([jnp.concatenate([xb[pl.ds(1, nz - 1), h, c * HALF + i * KC + j].reshape(zr, y) for j in range(KC)])
                  for c in range(2) for h in range(2)])
        out = _mm(_split(x), [wysp[m] for m in range(3)])
        for k in range(nb):
            sf[ck(i), k, pl.ds(ZT, zr)] = out[:, k * y:(k + 1) * y].reshape(KC, zr, y)
        r[ck(i), pl.ds(b * zb + ZT, zr)] = sf[ck(i), b, pl.ds(ZT, zr)]
        for d in range(3):
            fwd(i, d).start()

    for c in loads[2:]:
        c.wait()
    split_table(wisp, 128)
    lane = lax.broadcasted_iota(jnp.int32, (n, y), 1)
    sign = jnp.where(lane < y // 2, 1.0, -1.0).astype(F32)

    @pl.loop(0, npiece)
    def _(i):
        for d in range(3):
            fwda(i, d).wait_recv()

    @pl.loop(0, nchunk)
    def _(i):
        for d in range(3):
            fwd(i, d).wait_recv()
        gload(i).wait()
        e = _dot(csv[...], _cat([r[i * KC + j] for j in range(KC)]))
        parts = []
        for j in range(KC):
            cols = slice(j * y, (j + 1) * y)
            g1 = gv[lax.rem(i, gs), j] * (1.0 / n)
            gt = jnp.transpose(jnp.concatenate([g1, g1], axis=0))
            parts.append((e[:n, cols] + sign * pltpu.roll(e[n:, cols], y // 2, 1)) * gt)

        @pl.when(i + gs < nchunk)
        def _():
            gload(i + gs).start()
        e = _dot(csv[...], _cat(parts))
        for j in range(KC):
            cols = slice(j * y, (j + 1) * y)
            r[i * KC + j] = e[:n, cols] - sign * pltpu.roll(e[n:, cols], y // 2, 1)
        v[ck(i), b] = r[ck(i), pl.ds(b * zb, zb)]
        for d in range(3):
            bwd(i, d).start()

    @pl.loop(0, nz)
    def _(z):
        xremote(z).wait_send()

    def yinverse(i):
        for d in range(3):
            bwd(i, d).wait_recv()
        out = _mm(_split(_cat([v[ck(i), k].reshape(KC * zb, y) for k in range(nb)])), [wisp[m] for m in range(3)])

        def tile(h, c, j):
            m = h * 2 + c
            return out[j * zb:(j + 1) * zb, m * y:(m + 1) * y].reshape(nz, ZT, y)

        for c in range(2):
            for j in range(KC):
                t0, t1 = tile(0, c, j), tile(1, c, j)
                qx[:, i, a, j * 2 + c] = jnp.where(a == 0, t0, t1)
                ps[:, i * 2 * KC + j * 2 + c] = jnp.where(a == 0, t1, t0)

    @pl.loop(0, nbulk)
    def _(i):
        yinverse(i)
        qremote(i).start()

    @pl.loop(0, nbulk)
    def _(i):
        qremote(i).wait_recv()

    qrows = nchunk * 4 * KC
    brows = nbulk * 4 * KC
    qflat = qx.reshape(nz * qrows * ZT, y)

    @pl.loop(0, nz)
    def _(zi):
        @pl.when(zi >= 2)
        def _():
            wstore(zi - 2).wait()
        for z in range(0, ZT, 2):
            rhs = _cat([qflat[pl.ds(zi * qrows * ZT + z + i, brows, stride=ZT), :] for i in range(2)])
            out = _dot(aiv[...], rhs)
            for i in range(2):
                ws[lax.rem(zi, 2), z + i] = out[:, i * y:(i + 1) * y]
        wstore(zi).start()

    @pl.loop(nbulk, nchunk)
    def _(i):
        yinverse(i)
        qlast(i).start()
        qlocal(i).start()

    for z in (nz - 2, nz - 1):
        wstore(z).wait()

    @pl.loop(0, npiece)
    def _(i):
        for d in range(3):
            fwda(i, d).wait_send()

    @pl.loop(0, nchunk)
    def _(i):
        for d in range(3):
            fwd(i, d).wait_send()
            bwd(i, d).wait_send()

    @pl.loop(0, nbulk)
    def _(i):
        qremote(i).wait_send()

    @pl.loop(nbulk, nchunk)
    def _(i):
        qlocal(i).wait()
        qlast(i).wait()


def _finish(t_ref, w_ref, q_ref, o_ref, wv, qv, ov, in_sem, q_sem, out_sem):
    nz, x, zt, y = ov.shape
    k = q_ref.shape[1]
    src = qv.reshape(nz * k * zt, y)
    dst = ov.reshape(nz * x * zt, y)

    def load(i):
        return pltpu.make_async_copy(w_ref.at[pl.ds(i * zt, zt)], wv.at[pl.ds(i * zt, zt)], in_sem.at[i])

    def qload(i):
        return pltpu.make_async_copy(q_ref.at[i], qv.at[i], q_sem.at[i])

    def store(i):
        return pltpu.make_async_copy(ov.at[i], o_ref.at[:, pl.ds(i * zt, zt)], out_sem.at[i])

    @pl.loop(0, nz)
    def _(i):
        qload(i).start()
        load(i).start()

    @pl.loop(0, nz)
    def _(i):
        qload(i).wait()
        load(i).wait()
        for z in range(0, zt, 2):
            hi, mid, lo = _split(_cat([src[pl.ds(i * k * zt + z + j, k, stride=zt), :] for j in range(2)]))
            rhs = jnp.concatenate([s.astype(F32) for s in (lo, mid, hi, mid, hi, hi)], axis=0).astype(BF16)
            out = jnp.dot(t_ref[...], rhs, preferred_element_type=F32)
            for j in range(2):
                dst[pl.ds(i * x * zt + z + j, x, stride=zt), :] = wv[i * zt + z + j] + out[:, j * y:(j + 1) * y]
        store(i).start()

    @pl.loop(0, nz)
    def _(i):
        store(i).wait()


def solution(mesh):
    na, nb = mesh.shape["a"], mesh.shape["b"]

    def local(u, g):
        n, ya, zb = u.shape
        nkx = g.shape[0]
        kx = nkx * na
        nchunk, npiece, nz = nkx // KC, nkx // KA, zb // ZT
        brows = (nchunk - NLAST) * 4 * KC
        tf, ti = _xforward(n, kx, na), _xinverse(n, kx, na)
        bulk = np.ascontiguousarray(ti[:, :brows])
        hi, mid, lo = _nsplit(ti[:, brows:])
        last = np.concatenate([hi, mid, lo, hi, mid, hi], axis=1)
        wy, wi = _ytables(n, nb)
        c, s = _trig(n, n, n)
        cs = np.concatenate([c, s]).astype(np.float32)
        ut = jnp.transpose(u, (0, 2, 1))
        anyspec = pl.BlockSpec(memory_space=pl.ANY)
        dma = pltpu.SemaphoreType.DMA
        vm = lambda *shape: pltpu.VMEM(shape, F32)
        acc, ql = pl.pallas_call(
            functools.partial(_spectral, nb), name="spectral",
            in_specs=[anyspec] * 7, out_specs=[anyspec] * 2,
            out_shape=[jax.ShapeDtypeStruct((zb, n, ya), F32),
                       jax.ShapeDtypeStruct((nz, NLAST, na, 2 * KC, ZT, ya), F32)],
            scratch_shapes=[
                vm(3, n, ZT, ya), vm(nz, na, ROWS, ZT, ya), vm(nz, ROWS, ZT, ya),
                vm(nkx, nb, zb, 128), vm(nkx, n, 128), vm(nkx, nb, zb, 128),
                vm(nz, nchunk, na, 2 * KC, ZT, ya), vm(2, ZT, n, ya), vm(2, KC, *g.shape[1:]),
                vm(*tf.shape), vm(*wy.shape), vm(*cs.shape), vm(*bulk.shape),
                pltpu.VMEM((3, *tf.shape), BF16), pltpu.VMEM((3, *wy.shape), BF16), pltpu.VMEM((3, *wi.shape), BF16),
                dma((5,)), dma((3,)), dma((2,)), dma((nz,)), dma((nz,)), dma((3, npiece)), dma((3, npiece)),
                dma((3, nchunk)), dma((3, nchunk)), dma((3, nchunk)), dma((3, nchunk)),
                dma((nchunk,)), dma((nchunk,)), dma((NLAST,)), dma((2,)),
            ],
            compiler_params=pltpu.CompilerParams(
                collective_id=0, has_side_effects=True, vmem_limit_bytes=67043328),
        )(ut, g, tf, wy, cs, wi, bulk)
        k = NLAST * na * 2 * KC
        w = pl.pallas_call(
            _finish, name="finish",
            in_specs=[pl.BlockSpec(memory_space=pltpu.VMEM), anyspec, anyspec], out_specs=anyspec,
            out_shape=jax.ShapeDtypeStruct((n, zb, ya), F32),
            scratch_shapes=[vm(zb, n, ya), vm(nz, k, ZT, ya), vm(nz, n, ZT, ya), dma((nz,)), dma((nz,)), dma((nz,))],
            compiler_params=pltpu.CompilerParams(vmem_limit_bytes=62 << 20),
        )(last, acc, ql.reshape(nz, k, ZT, ya))
        return jnp.transpose(w, (0, 2, 1))

    return jax.shard_map(local, mesh=mesh, in_specs=(P(None, "a", "b"), P("a", "b", None)), out_specs=P(None, "a", "b"), check_vma=False)
```

time: 934 us -> 208 us (0.22)
  local copies, waits for them, and re-layouts: 323 us -> 0 us
  blocking collectives: 239 us -> 0 us
  Pallas kernels: 0 us -> 208 us
  waiting for transfers between devices: 182 us -> 0 us
  matrix products: 156 us -> 0 us
  other arithmetic: 16.1 us -> 0 us
    all_to_all x3 -> x0, blocking collectives: 239 us -> none  [the longest x1 196 us: local(): x = lax.all_to_all(x, 'b', 2, 3, tiled=True)]
    pallas_call x0 -> x2, Pallas kernels: none -> 208 us  [the longest x1 199 us: local(): pl.pallas_call(functools.partial(_spectral, nb), name='spectral', in_spec...]
    all_to_all x1 -> x0, waiting for transfers between devices: 182 us -> none  [local(): x = lax.all_to_all(x, 'b', 3, 2, tiled=True)]
    dot_general x20 -> x0, matrix products: 156 us -> none  [the longest x4 43.7 us: _mm(): return jnp.dot(p, q, precision=HI, preferred_element_type=jnp.float32)]
    slice x8 -> x0, local copies, waits for them, and re-layouts: 87.1 us -> none  [the longest x4 44.2 us: _line(): x[0]]
    squeeze x10 -> x0, local copies, waits for them, and re-layouts: 83.5 us -> none  [the longest x5 41.9 us: _line(): x[0]]
    all_to_all x4 -> x0, local copies, waits for them, and re-layouts: 64.4 us -> none  [the longest x1 21.9 us: local(): x = lax.all_to_all(x, 'b', 2, 3, tiled=True)]
    another operation x6 -> x0, local copies, waits for them, and re-layouts: 60.9 us -> none  [the longest x3 43 us: _line(): jnp.stack([e(x[0], c) + sign * e(x[1], s), e(x[1], c) - sign * e(x[0], s)])]
  transfers between devices with their start and end apart: 1 -> 0, of which waited for: 1 -> 0; matrix products, arithmetic and copies ran while one was open for 0% -> 0% of each run, Pallas kernels for 0% -> 0%
where the time goes in v2:
time: 208 us
  Pallas kernels  208 us (100%)
    pallas_call x1, Pallas kernels, local(): pl.pallas_call(functools.partial(_spectral, nb), name='spectral', in_spec...  199 us
    pallas_call x1, Pallas kernels, local(): pl.pallas_call(_finish, name='finish', in_specs=[pl.BlockSpec(memory_spac...  8.13 us

profile of v2, /device:TPU:0, one launch (start us, length us, event | category | flops | bytes accessed | tf_op | source)
XLA Modules:
  0.0 207.6 jit_solution(16065113794648276724)
XLA Ops:
  0.0 199.4 %spectral.1 = (f32[64,256,128]{2,1,0:T(8,128)}, f32[8,2,2,10,8,128]{5,4,3,2,1,0:T(8,128)}) custom-call(f32[256,64,128]{2,1,0:T(8,128)} %bitcast.3, f32[65,64,256]{2,1,0:T(8,128)} %g_ref.1, f32[432,256]{1,0:T(8,128)} %constant.12.clone.t_ref, f32[512,512]{1,0:T(8,128)} %constant.13.clone.wy_ref, f32[512,256]{1,0:T(8,128)} %constant.14.clone.cs_ref, ...), custom_call_target="tpu_custom_call" | custom-call | tf_op jit(solution)/shard_map/spectral/pallas_call | solution.py:409
  199.4 8.1 %finish.1 = f32[256,64,128]{2,1,0:T(8,128)} custom-call(bf16[256,240]{1,0:T(8,128)(2,1)} %constant.17.clone.t_ref, f32[64,256,128]{2,1,0:T(8,128)} %get-tuple-element.7.w_ref, f32[8,40,8,128]{3,2,1,0:T(8,128)} %bitcast.4), custom_call_target="tpu_custom_call" | custom-call | tf_op jit(solution)/shard_map/finish/pallas_call | solution.py:428

commit v3 on v2

--- a/solution.py
+++ b/solution.py
@@ -18,6 +18,7 @@
 ROWS = 136
 HALF = ROWS // 2
 TROWS = 144
+NA = 2
 
 
 def _trig(n, rows, cols):
@@ -82,9 +83,9 @@
 
 
 def _spectral(nb, u_ref, g_ref, t_ref, wy_ref, cs_ref, wi_ref, ai_ref, acc_ref, ql_ref,
-              uv, xb, ps, sf, r, v, qx, ws, gv, tv, wv, csv, aiv, tsp, wysp, wisp,
+              uv, xb, ps, sf, r, v, gv, tv, wv, csv, aiv, tsp, wysp, wisp,
               load_sem, u_sem, g_sem, xa_send, xa_recv, fa_send, fa_recv, f_send, f_recv,
-              b_send, b_recv, q_send, q_recv, ql_sem, w_sem):
+              b_send, b_recv, q_send, q_recv):
     b, a = lax.axis_index("b"), lax.axis_index("a")
     other = 1 - a
     nkx = g_ref.shape[0]
@@ -94,6 +95,8 @@
     zb = n // nb
     nz = zb // ZT
     y = 128
+    za, zr = NA * ZT, zb - NA * ZT
+    npad = 2 * nkx - n // 2 - 1
     bx, by = lax.rem(b, 2), lax.div(b, 2)
     peers = [lax.rem(by + d // 2, 2) * 2 + lax.rem(bx + d % 2, 2) for d in (1, 2, 3)]
     us = uv.shape[0]
@@ -119,39 +122,55 @@
         return pltpu.make_async_remote_copy(
             ps.at[z], xb.at[z, a], xa_send.at[z], xa_recv.at[z], device_id=(b, other), device_id_type=MESH)
 
-    def fwda(i, d):
-        return pltpu.make_async_remote_copy(
-            sf.at[ka(i), peers[d], pl.ds(0, ZT)], r.at[ka(i), pl.ds(b * zb, ZT)],
-            fa_send.at[d, i], fa_recv.at[d, i], device_id=(peers[d], a), device_id_type=MESH)
-
-    def fwd(i, d):
-        return pltpu.make_async_remote_copy(
-            sf.at[ck(i), peers[d], pl.ds(ZT, zb - ZT)], r.at[ck(i), pl.ds(b * zb + ZT, zb - ZT)],
+    def fwda(e, i, d, k):
+        rows = pl.ds(i * KA, k)
+        return pltpu.make_async_remote_copy(
+            sf.at[rows, peers[d], pl.ds(e * ZT, ZT)], r.at[rows, pl.ds(b * zb + e * ZT, ZT)],
+            fa_send.at[d, e * npiece + i], fa_recv.at[d, e * npiece + i],
+            device_id=(peers[d], a), device_id_type=MESH)
+
+    def fwd(i, d, k):
+        rows = pl.ds(i * KC, k)
+        return pltpu.make_async_remote_copy(
+            sf.at[rows, peers[d], pl.ds(za, zr)], r.at[rows, pl.ds(b * zb + za, zr)],
             f_send.at[d, i], f_recv.at[d, i], device_id=(peers[d], a), device_id_type=MESH)
 
-    def bwd(i, d):
-        return pltpu.make_async_remote_copy(
-            r.at[ck(i), pl.ds(peers[d] * zb, zb)], v.at[ck(i), b], b_send.at[d, i], b_recv.at[d, i],
+    def bwd(i, d, k):
+        rows = pl.ds(i * KC, k)
+        return pltpu.make_async_remote_copy(
+            r.at[rows, pl.ds(peers[d] * zb, zb)], v.at[rows, b], b_send.at[d, i], b_recv.at[d, i],
             device_id=(peers[d], a), device_id_type=MESH)
+
+    def sized(short, full, act):
+        @pl.when(jnp.logical_not(short))
+        def _():
+            act(full)
+
+        @pl.when(short)
+        def _():
+            act(full - npad)
+
+    def each(i, full, last, act):
+        sized(jnp.logical_and(i == last, a == 1), full, lambda k: [act(d, k) for d in range(3)])
+
+    def eacha(i, act):
+        each(i, KA, npiece - 1, act)
+
+    def eachc(i, act):
+        each(i, KC, nchunk - 1, act)
 
     def qsrc(i):
         return ps.at[:, pl.ds(i * 2 * KC, 2 * KC)]
 
     def qremote(i):
         return pltpu.make_async_remote_copy(
-            qsrc(i), qx.at[:, i, a], q_send.at[i], q_recv.at[i], device_id=(b, other), device_id_type=MESH)
+            qsrc(i), acc_ref.at[:, pl.ds((i * 2 + a) * 2 * KC, 2 * KC)], q_send.at[i], q_recv.at[i],
+            device_id=(b, other), device_id_type=MESH)
 
     def qlast(i):
         return pltpu.make_async_remote_copy(
-            qsrc(i), ql_ref.at[:, i - nbulk, a], q_send.at[i], q_recv.at[i],
+            qsrc(i), ql_ref.at[:, pl.ds(((i - nbulk) * 2 + a) * 2 * KC, 2 * KC)], q_send.at[i], q_recv.at[i],
             device_id=(b, other), device_id_type=MESH)
-
-    def qlocal(i):
-        return pltpu.make_async_copy(qx.at[:, i, a], ql_ref.at[:, i - nbulk, a], ql_sem.at[i - nbulk])
-
-    def wstore(z):
-        return pltpu.make_async_copy(
-            ws.at[lax.rem(z, 2)], acc_ref.at[pl.ds(z * ZT, ZT)], w_sem.at[lax.rem(z, 2)])
 
     barrier = pltpu.get_barrier_semaphore()
     for dev in [(b, other)] + [(pb, a) for pb in peers]:
@@ -201,44 +220,50 @@
     loads[1].wait()
     split_table(wysp, 128)
     loads[2].start()
-    xremote(0).wait_recv()
-
-    @pl.loop(0, npiece)
-    def _(i):
-        x = _split(_cat([xb[0, h, pl.ds(c * HALF + i * KA, KA)].reshape(KA * ZT, y)
-                         for c in range(2) for h in range(2)]))
-        out = _mm(x, [wysp[m] for m in range(3)])
-        for k in range(nb):
-            sf[ka(i), k, pl.ds(0, ZT)] = out[:, k * y:(k + 1) * y].reshape(KA, ZT, y)
-        r[ka(i), pl.ds(b * zb, ZT)] = sf[ka(i), b, pl.ds(0, ZT)]
-        for d in range(3):
-            fwda(i, d).start()
-
-    @pl.loop(1, nz)
-    def _(z):
-        @pl.when(z + us - 1 < nz)
-        def _():
-            uload(z + us - 1).start()
-        uload(z).wait()
-        xblock(z, (1, 0))
-        xremote(z).start()
-
-    @pl.loop(1, nz)
+
+    @pl.loop(0, NA)
+    def _(e):
+        xremote(e).wait_recv()
+
+        @pl.loop(0, npiece)
+        def _(i):
+            x = _split(_cat([xb[e, h, pl.ds(c * HALF + i * KA, KA)].reshape(KA * ZT, y)
+                             for c in range(2) for h in range(2)]))
+            out = _mm(x, [wysp[m] for m in range(3)])
+            zrow = pl.multiple_of(e * ZT, ZT)
+            for k in range(nb):
+                sf[ka(i), k, pl.ds(zrow, ZT)] = out[:, k * y:(k + 1) * y].reshape(KA, ZT, y)
+            r[ka(i), pl.ds(b * zb + zrow, ZT)] = sf[ka(i), b, pl.ds(zrow, ZT)]
+            eacha(i, lambda d, k: fwda(e, i, d, k).start())
+
+        @pl.loop(1 + 2 * e, 3 + (nz - 3) * e)
+        def _(z):
+            @pl.when(z + us - 1 < nz)
+            def _():
+                uload(z + us - 1).start()
+            uload(z).wait()
+            xblock(z, (1, 0))
+            xremote(z).start()
+
+    @pl.loop(NA, nz)
     def _(z):
         xremote(z).wait_recv()
 
-    zr = zb - ZT
-
     @pl.loop(0, nchunk)
     def _(i):
-        x = _cat([jnp.concatenate([xb[pl.ds(1, nz - 1), h, c * HALF + i * KC + j].reshape(zr, y) for j in range(KC)])
+        x = _cat([jnp.concatenate([xb[pl.ds(NA, nz - NA), h, c * HALF + i * KC + j].reshape(zr, y) for j in range(KC)])
                   for c in range(2) for h in range(2)])
         out = _mm(_split(x), [wysp[m] for m in range(3)])
         for k in range(nb):
-            sf[ck(i), k, pl.ds(ZT, zr)] = out[:, k * y:(k + 1) * y].reshape(KC, zr, y)
-        r[ck(i), pl.ds(b * zb + ZT, zr)] = sf[ck(i), b, pl.ds(ZT, zr)]
-        for d in range(3):
-            fwd(i, d).start()
+            sf[ck(i), k, pl.ds(za, zr)] = out[:, k * y:(k + 1) * y].reshape(KC, zr, y)
+        r[ck(i), pl.ds(b * zb + za, zr)] = sf[ck(i), b, pl.ds(za, zr)]
+        eachc(i, lambda d, k: fwd(i, d, k).start())
+
+    @pl.when(a == 1)
+    def _():
+        for k in range(npad):
+            r[nkx - 1 - k] = jnp.zeros((n, y), F32)
+            v[nkx - 1 - k] = jnp.zeros((nb, zb, y), F32)
 
     for c in loads[2:]:
         c.wait()
@@ -246,15 +271,15 @@
     lane = lax.broadcasted_iota(jnp.int32, (n, y), 1)
     sign = jnp.where(lane < y // 2, 1.0, -1.0).astype(F32)
 
-    @pl.loop(0, npiece)
-    def _(i):
-        for d in range(3):
-            fwda(i, d).wait_recv()
+    @pl.loop(0, NA)
+    def _(e):
+        @pl.loop(0, npiece)
+        def _(i):
+            eacha(i, lambda d, k: fwda(e, i, d, k).wait_recv())
 
     @pl.loop(0, nchunk)
     def _(i):
-        for d in range(3):
-            fwd(i, d).wait_recv()
+        eachc(i, lambda d, k: fwd(i, d, k).wait_recv())
         gload(i).wait()
         e = _dot(csv[...], _cat([r[i * KC + j] for j in range(KC)]))
         parts = []
@@ -272,16 +297,14 @@
             cols = slice(j * y, (j + 1) * y)
             r[i * KC + j] = e[:n, cols] - sign * pltpu.roll(e[n:, cols], y // 2, 1)
         v[ck(i), b] = r[ck(i), pl.ds(b * zb, zb)]
-        for d in range(3):
-            bwd(i, d).start()
+        eachc(i, lambda d, k: bwd(i, d, k).start())
 
     @pl.loop(0, nz)
     def _(z):
         xremote(z).wait_send()
 
-    def yinverse(i):
-        for d in range(3):
-            bwd(i, d).wait_recv()
+    def yinverse(i, own_ref, row):
+        eachc(i, lambda d, k: bwd(i, d, k).wait_recv())
         out = _mm(_split(_cat([v[ck(i), k].reshape(KC * zb, y) for k in range(nb)])), [wisp[m] for m in range(3)])
 
         def tile(h, c, j):
@@ -291,53 +314,44 @@
         for c in range(2):
             for j in range(KC):
                 t0, t1 = tile(0, c, j), tile(1, c, j)
-                qx[:, i, a, j * 2 + c] = jnp.where(a == 0, t0, t1)
+                own_ref[:, row + j * 2 + c] = jnp.where(a == 0, t0, t1)
                 ps[:, i * 2 * KC + j * 2 + c] = jnp.where(a == 0, t1, t0)
 
     @pl.loop(0, nbulk)
     def _(i):
-        yinverse(i)
+        yinverse(i, acc_ref, (i * 2 + a) * 2 * KC)
         qremote(i).start()
 
     @pl.loop(0, nbulk)
     def _(i):
         qremote(i).wait_recv()
 
-    qrows = nchunk * 4 * KC
     brows = nbulk * 4 * KC
-    qflat = qx.reshape(nz * qrows * ZT, y)
+    arows = acc_ref.shape[1]
+    flat = acc_ref.reshape(nz * arows * ZT, y)
 
     @pl.loop(0, nz)
     def _(zi):
-        @pl.when(zi >= 2)
-        def _():
-            wstore(zi - 2).wait()
         for z in range(0, ZT, 2):
-            rhs = _cat([qflat[pl.ds(zi * qrows * ZT + z + i, brows, stride=ZT), :] for i in range(2)])
+            rhs = _cat([flat[pl.ds(zi * arows * ZT + z + i, brows, stride=ZT), :] for i in range(2)])
             out = _dot(aiv[...], rhs)
             for i in range(2):
-                ws[lax.rem(zi, 2), z + i] = out[:, i * y:(i + 1) * y]
-        wstore(zi).start()
+                flat[pl.ds(zi * arows * ZT + z + i, arows, stride=ZT), :] = out[:, i * y:(i + 1) * y]
 
     @pl.loop(nbulk, nchunk)
     def _(i):
-        yinverse(i)
+        yinverse(i, ql_ref, ((i - nbulk) * 2 + a) * 2 * KC)
         qlast(i).start()
-        qlocal(i).start()
-
-    for z in (nz - 2, nz - 1):
-        wstore(z).wait()
-
-    @pl.loop(0, npiece)
-    def _(i):
-        for d in range(3):
-            fwda(i, d).wait_send()
+
+    @pl.loop(0, NA)
+    def _(e):
+        @pl.loop(0, npiece)
+        def _(i):
+            eacha(i, lambda d, k: fwda(e, i, d, k).wait_send())
 
     @pl.loop(0, nchunk)
     def _(i):
-        for d in range(3):
-            fwd(i, d).wait_send()
-            bwd(i, d).wait_send()
+        eachc(i, lambda d, k: (fwd(i, d, k).wait_send(), bwd(i, d, k).wait_send()))
 
     @pl.loop(0, nbulk)
     def _(i):
@@ -345,40 +359,28 @@
 
     @pl.loop(nbulk, nchunk)
     def _(i):
-        qlocal(i).wait()
         qlast(i).wait()
 
 
-def _finish(t_ref, w_ref, q_ref, o_ref, wv, qv, ov, in_sem, q_sem, out_sem):
+def _finish(t_ref, w_ref, q_ref, o_ref, ov, out_sem):
     nz, x, zt, y = ov.shape
     k = q_ref.shape[1]
-    src = qv.reshape(nz * k * zt, y)
+    src = q_ref.reshape(nz * k * zt, y)
+    acc = w_ref.reshape(nz * x * zt, y)
     dst = ov.reshape(nz * x * zt, y)
-
-    def load(i):
-        return pltpu.make_async_copy(w_ref.at[pl.ds(i * zt, zt)], wv.at[pl.ds(i * zt, zt)], in_sem.at[i])
-
-    def qload(i):
-        return pltpu.make_async_copy(q_ref.at[i], qv.at[i], q_sem.at[i])
 
     def store(i):
         return pltpu.make_async_copy(ov.at[i], o_ref.at[:, pl.ds(i * zt, zt)], out_sem.at[i])
 
     @pl.loop(0, nz)
     def _(i):
-        qload(i).start()
-        load(i).start()
-
-    @pl.loop(0, nz)
-    def _(i):
-        qload(i).wait()
-        load(i).wait()
         for z in range(0, zt, 2):
             hi, mid, lo = _split(_cat([src[pl.ds(i * k * zt + z + j, k, stride=zt), :] for j in range(2)]))
             rhs = jnp.concatenate([s.astype(F32) for s in (lo, mid, hi, mid, hi, hi)], axis=0).astype(BF16)
             out = jnp.dot(t_ref[...], rhs, preferred_element_type=F32)
             for j in range(2):
-                dst[pl.ds(i * x * zt + z + j, x, stride=zt), :] = wv[i * zt + z + j] + out[:, j * y:(j + 1) * y]
+                rows = pl.ds(i * x * zt + z + j, x, stride=zt)
+                dst[rows, :] = acc[rows, :] + out[:, j * y:(j + 1) * y]
         store(i).start()
 
     @pl.loop(0, nz)
@@ -394,6 +396,7 @@
         nkx = g.shape[0]
         kx = nkx * na
         nchunk, npiece, nz = nkx // KC, nkx // KA, zb // ZT
+        klast = NLAST * na * 2 * KC
         brows = (nchunk - NLAST) * 4 * KC
         tf, ti = _xforward(n, kx, na), _xinverse(n, kx, na)
         bulk = np.ascontiguousarray(ti[:, :brows])
@@ -404,34 +407,33 @@
         cs = np.concatenate([c, s]).astype(np.float32)
         ut = jnp.transpose(u, (0, 2, 1))
         anyspec = pl.BlockSpec(memory_space=pl.ANY)
+        vmspec = pl.BlockSpec(memory_space=pltpu.VMEM)
         dma = pltpu.SemaphoreType.DMA
         vm = lambda *shape: pltpu.VMEM(shape, F32)
         acc, ql = pl.pallas_call(
             functools.partial(_spectral, nb), name="spectral",
-            in_specs=[anyspec] * 7, out_specs=[anyspec] * 2,
-            out_shape=[jax.ShapeDtypeStruct((zb, n, ya), F32),
-                       jax.ShapeDtypeStruct((nz, NLAST, na, 2 * KC, ZT, ya), F32)],
+            in_specs=[pl.BlockSpec(memory_space=pltpu.HBM)] * 7, out_specs=[vmspec] * 2,
+            out_shape=[vm(nz, n, ZT, ya), vm(nz, klast, ZT, ya)],
             scratch_shapes=[
                 vm(3, n, ZT, ya), vm(nz, na, ROWS, ZT, ya), vm(nz, ROWS, ZT, ya),
                 vm(nkx, nb, zb, 128), vm(nkx, n, 128), vm(nkx, nb, zb, 128),
-                vm(nz, nchunk, na, 2 * KC, ZT, ya), vm(2, ZT, n, ya), vm(2, KC, *g.shape[1:]),
+                vm(2, KC, *g.shape[1:]),
                 vm(*tf.shape), vm(*wy.shape), vm(*cs.shape), vm(*bulk.shape),
                 pltpu.VMEM((3, *tf.shape), BF16), pltpu.VMEM((3, *wy.shape), BF16), pltpu.VMEM((3, *wi.shape), BF16),
-                dma((5,)), dma((3,)), dma((2,)), dma((nz,)), dma((nz,)), dma((3, npiece)), dma((3, npiece)),
+                dma((5,)), dma((3,)), dma((2,)), dma((nz,)), dma((nz,)), dma((3, NA * npiece)), dma((3, NA * npiece)),
                 dma((3, nchunk)), dma((3, nchunk)), dma((3, nchunk)), dma((3, nchunk)),
-                dma((nchunk,)), dma((nchunk,)), dma((NLAST,)), dma((2,)),
+                dma((nchunk,)), dma((nchunk,)),
             ],
             compiler_params=pltpu.CompilerParams(
-                collective_id=0, has_side_effects=True, vmem_limit_bytes=67043328),
+                collective_id=0, has_side_effects=True, vmem_limit_bytes=52 << 20),
         )(ut, g, tf, wy, cs, wi, bulk)
-        k = NLAST * na * 2 * KC
         w = pl.pallas_call(
             _finish, name="finish",
-            in_specs=[pl.BlockSpec(memory_space=pltpu.VMEM), anyspec, anyspec], out_specs=anyspec,
+            in_specs=[vmspec] * 3, out_specs=anyspec,
             out_shape=jax.ShapeDtypeStruct((n, zb, ya), F32),
-            scratch_shapes=[vm(zb, n, ya), vm(nz, k, ZT, ya), vm(nz, n, ZT, ya), dma((nz,)), dma((nz,)), dma((nz,))],
-            compiler_params=pltpu.CompilerParams(vmem_limit_bytes=62 << 20),
-        )(last, acc, ql.reshape(nz, k, ZT, ya))
+            scratch_shapes=[vm(nz, n, ZT, ya), dma((nz,))],
+            compiler_params=pltpu.CompilerParams(vmem_limit_bytes=24 << 20),
+        )(last, acc, ql)
         return jnp.transpose(w, (0, 2, 1))
 
     return jax.shard_map(local, mesh=mesh, in_specs=(P(None, "a", "b"), P("a", "b", None)), out_specs=P(None, "a", "b"), check_vma=False)

time: 208 us -> 202 us (0.971)
  Pallas kernels: 208 us -> 202 us
    pallas_call x1, Pallas kernels: 8.13 us -> 4.85 us  [local(): pl.pallas_call(_finish, name='finish', in_specs=[vmspec] * 3, out_specs=a...]
    pallas_call x1, Pallas kernels: 199 us -> 197 us  [local(): pl.pallas_call(functools.partial(_spectral, nb), name='spectral', in_spec...]
where the time goes in v3:
time: 202 us
  Pallas kernels  202 us (100%)
    pallas_call x1, Pallas kernels, local(): pl.pallas_call(functools.partial(_spectral, nb), name='spectral', in_spec...  197 us
    pallas_call x1, Pallas kernels, local(): pl.pallas_call(_finish, name='finish', in_specs=[vmspec] * 3, out_specs=a...  4.85 us

profile of v3, /device:TPU:0, one launch (start us, length us, event | category | flops | bytes accessed | tf_op | source)
XLA Modules:
  0.0 201.7 jit_solution(16118815199225748813)
XLA Ops:
  0.0 0.0 copy-start
  0.0 196.8 %spectral.1 = (f32[8,256,8,128]{3,2,1,0:T(8,128)S(1)}, f32[8,40,8,128]{3,2,1,0:T(8,128)S(1)}) custom-call(f32[256,64,128]{2,1,0:T(8,128)} %bitcast.2, f32[65,64,256]{2,1,0:T(8,128)} %g_ref.1, f32[432,256]{1,0:T(8,128)} %constant.12.clone.t_ref, f32[512,512]{1,0:T(8,128)} %constant.13.clone.wy_ref, f32[512,256]{1,0:T(8,128)} %constant.14.clone.cs_ref, ...), custom_call_target="tpu_custom_call" | custom-call | tf_op jit(solution)/shard_map/spectral/pallas_call | solution.py:413
  196.8 0.0 copy-done
  196.8 4.8 %finish.1 = f32[256,64,128]{2,1,0:T(8,128)} custom-call(bf16[256,240]{1,0:T(8,128)(2,1)S(1)} %copy-done, f32[8,256,8,128]{3,2,1,0:T(8,128)S(1)} %get-tuple-element.7.w_ref, f32[8,40,8,128]{3,2,1,0:T(8,128)S(1)} %get-tuple-element.8.q_ref), custom_call_target="tpu_custom_call" | custom-call | tf_op jit(solution)/shard_map/finish/pallas_call | solution.py:430
Async XLA Ops:
  0.0 196.8 %copy-start = (bf16[256,240]{1,0:T(8,128)(2,1)S(1)}, bf16[256,240]{1,0:T(8,128)(2,1)}, u32[]{:S(2)}) copy-start(bf16[256,240]{1,0:T(8,128)(2,1)} %constant.17.clone.t_ref) | copy-start | bytes 368644

commit v4 on v3

--- a/solution.py
+++ b/solution.py
@@ -13,12 +13,13 @@
 MESH = pl.DeviceIdType.MESH
 KC = 5
 KA = 13
-NLAST = 2
+NLAST = 4
 ZT = 8
 ROWS = 136
-HALF = ROWS // 2
 TROWS = 144
 NA = 2
+NS = 2
+SL = 8
 
 
 def _trig(n, rows, cols):
@@ -31,10 +32,8 @@
 def _xforward(n, kx, na):
     cx, sx = _trig(n, kx, n)
     keep = (np.arange(kx) <= n // 2).astype(np.float64)[:, None]
-    t = np.zeros((na, 2, HALF, n))
-    t[:, 0, : kx // na] = (cx * keep).reshape(na, kx // na, n)
-    t[:, 1, : kx // na] = (-sx * keep).reshape(na, kx // na, n)
-    t = np.pad(t.reshape(na, ROWS, n), ((0, 0), (0, TROWS - ROWS), (0, 0)))
+    t = np.stack([cx * keep, -sx * keep]).reshape(2, na, -1, KA, n).transpose(1, 2, 0, 3, 4).reshape(na, -1, n)
+    t = np.pad(t, ((0, 0), (0, TROWS - t.shape[1]), (0, 0)))
     return np.concatenate([t, t[:1]]).reshape((na + 1) * TROWS, n).astype(np.float32)
 
 
@@ -42,8 +41,10 @@
     cx, sx = _trig(n, kx, n)
     k = np.arange(kx)
     wgt = (np.where((k == 0) | (k == n // 2), 1.0, 2.0) * (k <= n // 2) / n)[:, None]
-    t = np.stack([cx * wgt, -sx * wgt], 1).reshape(na, kx // na // KC, KC, 2, n)
-    return t.transpose(1, 0, 2, 3, 4).reshape(2 * kx, n).T.astype(np.float32).copy()
+    t = np.stack([cx * wgt, -sx * wgt], 1).reshape(na, kx // na, 2 * n)
+    ends = list(range(0, kx // na - NS * KC + 1, KC)) + [kx // na]
+    t = np.concatenate([t[:, i:j].reshape(-1, n) for i, j in zip(ends, ends[1:])])
+    return t.T.astype(np.float32).copy()
 
 
 def _ytables(n, nb):
@@ -82,10 +83,20 @@
     return jnp.concatenate(parts, axis=1)
 
 
-def _spectral(nb, u_ref, g_ref, t_ref, wy_ref, cs_ref, wi_ref, ai_ref, acc_ref, ql_ref,
-              uv, xb, ps, sf, r, v, gv, tv, wv, csv, aiv, tsp, wysp, wisp,
+def _add_last(t_ref, q_ref, qrow, k, acc_ref, row, dst_ref, drow, x):
+    for z in range(0, ZT, 2):
+        hi, mid, lo = _split(_cat([q_ref[pl.ds(qrow + z + j, k, stride=ZT), :] for j in range(2)]))
+        rhs = jnp.concatenate([s.astype(F32) for s in (lo, mid, hi, mid, hi, hi)], axis=0).astype(BF16)
+        out = jnp.dot(t_ref[...], rhs, preferred_element_type=F32)
+        for j in range(2):
+            part = acc_ref[pl.ds(row + z + j, x, stride=ZT), :] + out[:, j * 128:(j + 1) * 128]
+            dst_ref[pl.ds(drow + z + j, x, stride=ZT), :] = part
+
+
+def _spectral(nb, u_ref, g_ref, t_ref, wy_ref, cs_ref, wi_ref, ai_ref, al_ref, acc_ref, ql_ref,
+              uv, xb, ps, sf, r, v, gv, tv, wv, csv, aiv, tsp, wysp, wisp, alv,
               load_sem, u_sem, g_sem, xa_send, xa_recv, fa_send, fa_recv, f_send, f_recv,
-              b_send, b_recv, q_send, q_recv):
+              b_send, b_recv, q_send, q_recv, xp_send, xp_recv):
     b, a = lax.axis_index("b"), lax.axis_index("a")
     other = 1 - a
     nkx = g_ref.shape[0]
@@ -108,7 +119,7 @@
         return pl.ds(i * KA, KA)
 
     loads = [pltpu.make_async_copy(s, d, load_sem.at[i]) for i, (s, d) in enumerate(
-        [(t_ref, tv), (wy_ref, wv), (wi_ref, wv), (cs_ref, csv), (ai_ref, aiv)])]
+        [(t_ref, tv), (wy_ref, wv), (wi_ref, wv), (cs_ref, csv), (ai_ref, aiv), (al_ref, alv)])]
     gs = gv.shape[0]
 
     def gload(i):
@@ -122,6 +133,12 @@
         return pltpu.make_async_remote_copy(
             ps.at[z], xb.at[z, a], xa_send.at[z], xa_recv.at[z], device_id=(b, other), device_id_type=MESH)
 
+    def xpiece(i):
+        rows = pl.ds(i * 2 * KA, 2 * KA)
+        return pltpu.make_async_remote_copy(
+            ps.at[0, rows], xb.at[0, a, rows], xp_send.at[i], xp_recv.at[i],
+            device_id=(b, other), device_id_type=MESH)
+
     def fwda(e, i, d, k):
         rows = pl.ds(i * KA, k)
         return pltpu.make_async_remote_copy(
@@ -139,6 +156,18 @@
         rows = pl.ds(i * KC, k)
         return pltpu.make_async_remote_copy(
             r.at[rows, pl.ds(peers[d] * zb, zb)], v.at[rows, b], b_send.at[d, i], b_recv.at[d, i],
+            device_id=(peers[d], a), device_id_type=MESH)
+
+    zs, nzi = zb // SL, nz // SL
+    nwhole, nk = nchunk - NS, NS * KC
+    k0 = nkx - nk
+    qlrow = (nwhole - nbulk) * 4 * KC + a * 2 * nk
+
+    def bwdl(p, d, k):
+        rows = pl.ds(k0, k)
+        return pltpu.make_async_remote_copy(
+            r.at[rows, pl.ds(peers[d] * zb + p * zs, zs)], v.at[rows, b, pl.ds(p * zs, zs)],
+            b_send.at[d, nwhole + p], b_recv.at[d, nwhole + p],
             device_id=(peers[d], a), device_id_type=MESH)
 
     def sized(short, full, act):
@@ -168,20 +197,22 @@
             device_id=(b, other), device_id_type=MESH)
 
     def qlast(i):
-        return pltpu.make_async_remote_copy(
-            qsrc(i), ql_ref.at[:, pl.ds(((i - nbulk) * 2 + a) * 2 * KC, 2 * KC)], q_send.at[i], q_recv.at[i],
-            device_id=(b, other), device_id_type=MESH)
+        rows = pl.ds(((i - nbulk) * 2 + a) * 2 * KC, 2 * KC)
+        return pltpu.make_async_remote_copy(
+            qsrc(i), ql_ref.at[:, rows], q_send.at[i], q_recv.at[i], device_id=(b, other), device_id_type=MESH)
+
+    def qslice(p):
+        zi = pl.ds(p * nzi, nzi)
+        return pltpu.make_async_remote_copy(
+            ps.at[zi, pl.ds(k0 * 2, nk * 2)], ql_ref.at[zi, pl.ds(qlrow, nk * 2)],
+            q_send.at[nwhole + p], q_recv.at[nwhole + p], device_id=(b, other), device_id_type=MESH)
 
     barrier = pltpu.get_barrier_semaphore()
     for dev in [(b, other)] + [(pb, a) for pb in peers]:
         pl.semaphore_signal(barrier, inc=1, device_id=dev, device_id_type=MESH)
+    uload(0).start()
     loads[0].start()
-    for z in range(us):
-        uload(z).start()
-    for c in (loads[1], loads[3], loads[4]):
-        c.start()
-    for i in range(gs):
-        gload(i).start()
+    loads[1].start()
 
     src = uv.reshape(us * n * ZT, y)
     own = xb.reshape(nz * 2 * ROWS * ZT, y)
@@ -213,9 +244,19 @@
     for m, part in enumerate(_split(tv[...])):
         tsp[m] = part
     uload(0).wait()
+    for z in range(1, us):
+        uload(z).start()
+    for c in loads[3:]:
+        c.start()
+    for i in range(gs):
+        gload(i).start()
     xblock(0, (1,))
     pl.semaphore_wait(barrier, 4)
-    xremote(0).start()
+
+    @pl.loop(0, npiece)
+    def _(i):
+        xpiece(i).start()
+
     xblock(0, (0,))
     loads[1].wait()
     split_table(wysp, 128)
@@ -223,11 +264,16 @@
 
     @pl.loop(0, NA)
     def _(e):
-        xremote(e).wait_recv()
+        @pl.when(e > 0)
+        def _():
+            xremote(e).wait_recv()
 
         @pl.loop(0, npiece)
         def _(i):
-            x = _split(_cat([xb[e, h, pl.ds(c * HALF + i * KA, KA)].reshape(KA * ZT, y)
+            @pl.when(e == 0)
+            def _():
+                xpiece(i).wait_recv()
+            x = _split(_cat([xb[e, h, pl.ds((2 * i + c) * KA, KA)].reshape(KA * ZT, y)
                              for c in range(2) for h in range(2)]))
             out = _mm(x, [wysp[m] for m in range(3)])
             zrow = pl.multiple_of(e * ZT, ZT)
@@ -249,9 +295,12 @@
     def _(z):
         xremote(z).wait_recv()
 
+    def xrow(k, c):
+        return (lax.div(k, KA) * 2 + c) * KA + lax.rem(k, KA)
+
     @pl.loop(0, nchunk)
     def _(i):
-        x = _cat([jnp.concatenate([xb[pl.ds(NA, nz - NA), h, c * HALF + i * KC + j].reshape(zr, y) for j in range(KC)])
+        x = _cat([jnp.concatenate([xb[pl.ds(NA, nz - NA), h, xrow(i * KC + j, c)].reshape(zr, y) for j in range(KC)])
                   for c in range(2) for h in range(2)])
         out = _mm(_split(x), [wysp[m] for m in range(3)])
         for k in range(nb):
@@ -297,29 +346,45 @@
             cols = slice(j * y, (j + 1) * y)
             r[i * KC + j] = e[:n, cols] - sign * pltpu.roll(e[n:, cols], y // 2, 1)
         v[ck(i), b] = r[ck(i), pl.ds(b * zb, zb)]
-        eachc(i, lambda d, k: bwd(i, d, k).start())
-
-    @pl.loop(0, nz)
+
+        @pl.when(i < nwhole)
+        def _():
+            for d in range(3):
+                bwd(i, d, KC).start()
+
+    @pl.loop(0, SL)
+    def _(p):
+        sized(a == 1, nk, lambda k: [bwdl(p, d, k).start() for d in range(3)])
+
+    @pl.loop(0, npiece)
+    def _(i):
+        xpiece(i).wait_send()
+
+    @pl.loop(1, nz)
     def _(z):
         xremote(z).wait_send()
 
-    def yinverse(i, own_ref, row):
-        eachc(i, lambda d, k: bwd(i, d, k).wait_recv())
-        out = _mm(_split(_cat([v[ck(i), k].reshape(KC * zb, y) for k in range(nb)])), [wisp[m] for m in range(3)])
+    def yinverse(k, nk, own_ref, row, p, zs):
+        z0, nzi = pl.multiple_of(p * zs, ZT), zs // ZT
+        zi = pl.ds(p * nzi, nzi)
+        x = _cat([v[pl.ds(k, nk), m, pl.ds(z0, zs)].reshape(nk * zs, y) for m in range(nb)])
+        out = _mm(_split(x), [wisp[m] for m in range(3)])
 
         def tile(h, c, j):
             m = h * 2 + c
-            return out[j * zb:(j + 1) * zb, m * y:(m + 1) * y].reshape(nz, ZT, y)
+            return out[j * zs:(j + 1) * zs, m * y:(m + 1) * y].reshape(nzi, ZT, y)
 
         for c in range(2):
-            for j in range(KC):
+            for j in range(nk):
                 t0, t1 = tile(0, c, j), tile(1, c, j)
-                own_ref[:, row + j * 2 + c] = jnp.where(a == 0, t0, t1)
-                ps[:, i * 2 * KC + j * 2 + c] = jnp.where(a == 0, t1, t0)
+                own_ref[zi, row + j * 2 + c] = jnp.where(a == 0, t0, t1)
+                ps[zi, k * 2 + j * 2 + c] = jnp.where(a == 0, t1, t0)
 
     @pl.loop(0, nbulk)
     def _(i):
-        yinverse(i, acc_ref, (i * 2 + a) * 2 * KC)
+        for d in range(3):
+            bwd(i, d, KC).wait_recv()
+        yinverse(i * KC, KC, acc_ref, (i * 2 + a) * 2 * KC, 0, zb)
         qremote(i).start()
 
     @pl.loop(0, nbulk)
@@ -338,10 +403,33 @@
             for i in range(2):
                 flat[pl.ds(zi * arows * ZT + z + i, arows, stride=ZT), :] = out[:, i * y:(i + 1) * y]
 
-    @pl.loop(nbulk, nchunk)
-    def _(i):
-        yinverse(i, ql_ref, ((i - nbulk) * 2 + a) * 2 * KC)
+    @pl.loop(nbulk, nwhole)
+    def _(i):
+        for d in range(3):
+            bwd(i, d, KC).wait_recv()
+        yinverse(i * KC, KC, ql_ref, ((i - nbulk) * 2 + a) * 2 * KC, 0, zb)
         qlast(i).start()
+
+    krows = ql_ref.shape[1]
+    qflat = ql_ref.reshape(nz * krows * ZT, y)
+
+    @pl.loop(nbulk, nwhole)
+    def _(i):
+        qlast(i).wait_recv()
+
+    @pl.loop(0, SL)
+    def _(p):
+        sized(a == 1, nk, lambda k: [bwdl(p, d, k).wait_recv() for d in range(3)])
+        yinverse(k0, nk, ql_ref, qlrow, p, zs)
+        qslice(p).start()
+
+        @pl.when(p > 0)
+        def _():
+            qslice(p - 1).wait_recv()
+
+            @pl.loop((p - 1) * nzi, p * nzi)
+            def _(zi):
+                _add_last(alv, qflat, zi * krows * ZT, krows, flat, zi * arows * ZT, flat, zi * arows * ZT, arows)
 
     @pl.loop(0, NA)
     def _(e):
@@ -351,41 +439,50 @@
 
     @pl.loop(0, nchunk)
     def _(i):
-        eachc(i, lambda d, k: (fwd(i, d, k).wait_send(), bwd(i, d, k).wait_send()))
+        eachc(i, lambda d, k: fwd(i, d, k).wait_send())
+
+    @pl.loop(0, nwhole)
+    def _(i):
+        for d in range(3):
+            bwd(i, d, KC).wait_send()
 
     @pl.loop(0, nbulk)
     def _(i):
         qremote(i).wait_send()
 
-    @pl.loop(nbulk, nchunk)
-    def _(i):
-        qlast(i).wait()
+    @pl.loop(nbulk, nwhole)
+    def _(i):
+        qlast(i).wait_send()
+
+    @pl.loop(0, SL)
+    def _(p):
+        sized(a == 1, nk, lambda k: [bwdl(p, d, k).wait_send() for d in range(3)])
+        qslice(p).wait_send()
+
+    qslice(SL - 1).wait_recv()
 
 
 def _finish(t_ref, w_ref, q_ref, o_ref, ov, out_sem):
-    nz, x, zt, y = ov.shape
+    nz, x, zt, y = w_ref.shape
     k = q_ref.shape[1]
+    rest = ov.shape[0]
     src = q_ref.reshape(nz * k * zt, y)
     acc = w_ref.reshape(nz * x * zt, y)
-    dst = ov.reshape(nz * x * zt, y)
-
-    def store(i):
-        return pltpu.make_async_copy(ov.at[i], o_ref.at[:, pl.ds(i * zt, zt)], out_sem.at[i])
-
-    @pl.loop(0, nz)
-    def _(i):
-        for z in range(0, zt, 2):
-            hi, mid, lo = _split(_cat([src[pl.ds(i * k * zt + z + j, k, stride=zt), :] for j in range(2)]))
-            rhs = jnp.concatenate([s.astype(F32) for s in (lo, mid, hi, mid, hi, hi)], axis=0).astype(BF16)
-            out = jnp.dot(t_ref[...], rhs, preferred_element_type=F32)
-            for j in range(2):
-                rows = pl.ds(i * x * zt + z + j, x, stride=zt)
-                dst[rows, :] = acc[rows, :] + out[:, j * y:(j + 1) * y]
-        store(i).start()
-
-    @pl.loop(0, nz)
-    def _(i):
-        store(i).wait()
+    dst = ov.reshape(rest * x * zt, y)
+
+    def store(i, ref):
+        return pltpu.make_async_copy(ref, o_ref.at[:, pl.ds(i * zt, zt)], out_sem.at[i])
+
+    for i in range(nz - rest):
+        store(i, w_ref.at[i]).start()
+    for j in range(rest):
+        i = nz - rest + j
+        _add_last(t_ref, src, i * k * zt, k, acc, i * x * zt, dst, j * x * zt, x)
+        store(i, ov.at[j]).start()
+    for i in range(nz - rest):
+        store(i, w_ref.at[i]).wait()
+    for j in range(rest):
+        store(nz - rest + j, ov.at[j]).wait()
 
 
 def solution(mesh):
@@ -412,7 +509,7 @@
         vm = lambda *shape: pltpu.VMEM(shape, F32)
         acc, ql = pl.pallas_call(
             functools.partial(_spectral, nb), name="spectral",
-            in_specs=[pl.BlockSpec(memory_space=pltpu.HBM)] * 7, out_specs=[vmspec] * 2,
+            in_specs=[pl.BlockSpec(memory_space=pltpu.HBM)] * 8, out_specs=[vmspec] * 2,
             out_shape=[vm(nz, n, ZT, ya), vm(nz, klast, ZT, ya)],
             scratch_shapes=[
                 vm(3, n, ZT, ya), vm(nz, na, ROWS, ZT, ya), vm(nz, ROWS, ZT, ya),
@@ -420,18 +517,19 @@
                 vm(2, KC, *g.shape[1:]),
                 vm(*tf.shape), vm(*wy.shape), vm(*cs.shape), vm(*bulk.shape),
                 pltpu.VMEM((3, *tf.shape), BF16), pltpu.VMEM((3, *wy.shape), BF16), pltpu.VMEM((3, *wi.shape), BF16),
-                dma((5,)), dma((3,)), dma((2,)), dma((nz,)), dma((nz,)), dma((3, NA * npiece)), dma((3, NA * npiece)),
-                dma((3, nchunk)), dma((3, nchunk)), dma((3, nchunk)), dma((3, nchunk)),
-                dma((nchunk,)), dma((nchunk,)),
+                pltpu.VMEM(last.shape, BF16),
+                dma((6,)), dma((3,)), dma((2,)), dma((nz,)), dma((nz,)), dma((3, NA * npiece)), dma((3, NA * npiece)),
+                dma((3, nchunk)), dma((3, nchunk)), dma((3, nchunk + SL)), dma((3, nchunk + SL)),
+                dma((nchunk + SL,)), dma((nchunk + SL,)), dma((npiece,)), dma((npiece,)),
             ],
             compiler_params=pltpu.CompilerParams(
-                collective_id=0, has_side_effects=True, vmem_limit_bytes=52 << 20),
-        )(ut, g, tf, wy, cs, wi, bulk)
+                collective_id=0, has_side_effects=True, vmem_limit_bytes=53 << 20),
+        )(ut, g, tf, wy, cs, wi, bulk, last)
         w = pl.pallas_call(
             _finish, name="finish",
             in_specs=[vmspec] * 3, out_specs=anyspec,
             out_shape=jax.ShapeDtypeStruct((n, zb, ya), F32),
-            scratch_shapes=[vm(nz, n, ZT, ya), dma((nz,))],
+            scratch_shapes=[vm(nz // SL, n, ZT, ya), dma((nz,))],
             compiler_params=pltpu.CompilerParams(vmem_limit_bytes=24 << 20),
         )(last, acc, ql)
         return jnp.transpose(w, (0, 2, 1))

time: 202 us -> 200 us (0.990)
  no operation moved by 1% of the time
where the time goes in v4:
time: 200 us
  Pallas kernels  200 us (100%)
    pallas_call x1, Pallas kernels, local(): pl.pallas_call(functools.partial(_spectral, nb), name='spectral', in_spec...  196 us

profile of v4, /device:TPU:0, one launch (start us, length us, event | category | flops | bytes accessed | tf_op | source)
XLA Modules:
  0.0 199.8 jit_solution(6037097037625565670)
XLA Ops:
  0.0 0.0 copy-start
  0.0 196.4 %spectral.1 = (f32[8,256,8,128]{3,2,1,0:T(8,128)S(1)}, f32[8,80,8,128]{3,2,1,0:T(8,128)S(1)}) custom-call(f32[256,64,128]{2,1,0:T(8,128)} %bitcast.2, f32[65,64,256]{2,1,0:T(8,128)} %g_ref.1, f32[432,256]{1,0:T(8,128)} %constant.12.clone.t_ref, f32[512,512]{1,0:T(8,128)} %constant.13.clone.wy_ref, f32[512,256]{1,0:T(8,128)} %constant.14.clone.cs_ref, ...), custom_call_target="tpu_custom_call" | custom-call | tf_op jit(solution)/shard_map/spectral/pallas_call | solution.py:510
  196.4 0.0 copy-done
  196.4 3.4 %finish.1 = f32[256,64,128]{2,1,0:T(8,128)} custom-call(bf16[256,480]{1,0:T(8,128)(2,1)S(1)} %copy-done, f32[8,256,8,128]{3,2,1,0:T(8,128)S(1)} %get-tuple-element.7.w_ref, f32[8,80,8,128]{3,2,1,0:T(8,128)S(1)} %get-tuple-element.8.q_ref), custom_call_target="tpu_custom_call" | custom-call | tf_op jit(solution)/shard_map/finish/pallas_call | solution.py:528
Async XLA Ops:
  0.0 196.4 %copy-start = (bf16[256,480]{1,0:T(8,128)(2,1)S(1)}, bf16[256,480]{1,0:T(8,128)(2,1)}, u32[]{:S(2)}) copy-start(bf16[256,480]{1,0:T(8,128)(2,1)} %constant.17.clone.al_ref.t_ref) | copy-start | bytes 737284

commit v5 on v4

--- a/solution.py
+++ b/solution.py
@@ -18,7 +18,7 @@
 ROWS = 136
 TROWS = 144
 NA = 2
-NS = 2
+NS = 3
 SL = 8
 
 

time: 200 us -> 199 us (level)
  no operation moved by 1% of the time
where the time goes in v5:
time: 199 us
  Pallas kernels  199 us (100%)
    pallas_call x1, Pallas kernels, local(): pl.pallas_call(functools.partial(_spectral, nb), name='spectral', in_spec...  195 us

profile of v5, /device:TPU:0, one launch (start us, length us, event | category | flops | bytes accessed | tf_op | source)
XLA Modules:
  0.0 198.7 jit_solution(12376033225300431762)
XLA Ops:
  0.0 0.0 copy-start
  0.0 195.3 %spectral.1 = (f32[8,256,8,128]{3,2,1,0:T(8,128)S(1)}, f32[8,80,8,128]{3,2,1,0:T(8,128)S(1)}) custom-call(f32[256,64,128]{2,1,0:T(8,128)} %bitcast.2, f32[65,64,256]{2,1,0:T(8,128)} %g_ref.1, f32[432,256]{1,0:T(8,128)} %constant.12.clone.t_ref, f32[512,512]{1,0:T(8,128)} %constant.13.clone.wy_ref, f32[512,256]{1,0:T(8,128)} %constant.14.clone.cs_ref, ...), custom_call_target="tpu_custom_call" | custom-call | tf_op jit(solution)/shard_map/spectral/pallas_call | solution.py:510
  195.3 0.0 copy-done
  195.4 3.4 %finish.1 = f32[256,64,128]{2,1,0:T(8,128)} custom-call(bf16[256,480]{1,0:T(8,128)(2,1)S(1)} %copy-done, f32[8,256,8,128]{3,2,1,0:T(8,128)S(1)} %get-tuple-element.7.w_ref, f32[8,80,8,128]{3,2,1,0:T(8,128)S(1)} %get-tuple-element.8.q_ref), custom_call_target="tpu_custom_call" | custom-call | tf_op jit(solution)/shard_map/finish/pallas_call | solution.py:528
Async XLA Ops:
  0.0 195.3 %copy-start = (bf16[256,480]{1,0:T(8,128)(2,1)S(1)}, bf16[256,480]{1,0:T(8,128)(2,1)}, u32[]{:S(2)}) copy-start(bf16[256,480]{1,0:T(8,128)(2,1)} %constant.17.clone.al_ref.t_ref) | copy-start | bytes 737284

commit v6 on v5

--- a/solution.py
+++ b/solution.py
@@ -109,7 +109,7 @@
     za, zr = NA * ZT, zb - NA * ZT
     npad = 2 * nkx - n // 2 - 1
     bx, by = lax.rem(b, 2), lax.div(b, 2)
-    peers = [lax.rem(by + d // 2, 2) * 2 + lax.rem(bx + d % 2, 2) for d in (1, 2, 3)]
+    peers = [lax.rem(by + d // 2, 2) * 2 + lax.rem(bx + d % 2, 2) for d in (3, 1, 2)]
     us = uv.shape[0]
 
     def ck(i):

time: 199 us -> 198 us (level)
  no operation moved by 1% of the time
where the time goes in v6:
time: 198 us
  Pallas kernels  198 us (100%)
    pallas_call x1, Pallas kernels, local(): pl.pallas_call(functools.partial(_spectral, nb), name='spectral', in_spec...  195 us

profile of v6, /device:TPU:0, one launch (start us, length us, event | category | flops | bytes accessed | tf_op | source)
XLA Modules:
  0.0 198.0 jit_solution(12179964485480627490)
XLA Ops:
  0.0 0.0 copy-start
  0.0 194.6 %spectral.1 = (f32[8,256,8,128]{3,2,1,0:T(8,128)S(1)}, f32[8,80,8,128]{3,2,1,0:T(8,128)S(1)}) custom-call(f32[256,64,128]{2,1,0:T(8,128)} %bitcast.2, f32[65,64,256]{2,1,0:T(8,128)} %g_ref.1, f32[432,256]{1,0:T(8,128)} %constant.12.clone.t_ref, f32[512,512]{1,0:T(8,128)} %constant.13.clone.wy_ref, f32[512,256]{1,0:T(8,128)} %constant.14.clone.cs_ref, ...), custom_call_target="tpu_custom_call" | custom-call | tf_op jit(solution)/shard_map/spectral/pallas_call | solution.py:510
  194.6 0.0 copy-done
  194.7 3.4 %finish.1 = f32[256,64,128]{2,1,0:T(8,128)} custom-call(bf16[256,480]{1,0:T(8,128)(2,1)S(1)} %copy-done, f32[8,256,8,128]{3,2,1,0:T(8,128)S(1)} %get-tuple-element.7.w_ref, f32[8,80,8,128]{3,2,1,0:T(8,128)S(1)} %get-tuple-element.8.q_ref), custom_call_target="tpu_custom_call" | custom-call | tf_op jit(solution)/shard_map/finish/pallas_call | solution.py:528
Async XLA Ops:
  0.0 194.6 %copy-start = (bf16[256,480]{1,0:T(8,128)(2,1)S(1)}, bf16[256,480]{1,0:T(8,128)(2,1)}, u32[]{:S(2)}) copy-start(bf16[256,480]{1,0:T(8,128)(2,1)} %constant.17.clone.al_ref.t_ref) | copy-start | bytes 737284
